TPU v7x, 32 devices: a whole 2x2x4 slice. The times are simulated.
32 devices in a mesh: rep: 4 (over y, core), grp: 8 (over z, x).
Axes of the slice: x: 2, y: 2, z: 4, core: 2. Of those that a mesh axis runs over, the one named last changes fastest.
Arguments:
- hidden_in: bfloat16 [128, 7168], P(('rep', 'grp')), may hold values from -3 to 3
- q_nope: bfloat16 [128, 8192], P(('rep', 'grp')), may hold values from -9 to 9
- q_rope: bfloat16 [128, 4096], P(('rep', 'grp')), may hold values from -36 to 36
- new_kv: bfloat16 [128, 576], P(('rep', 'grp')), may hold values from -6 to 6
- cache_kv: bfloat16 [128, 4096, 576], P(('rep', 'grp')), may hold values from -10 to 10
- lengths: int32 [128], P(('rep', 'grp')), may hold values from 2 to 4096, as said below
- w_uk: bfloat16 [512, 8192], P('rep'), may hold values from -0.5 to 0.5
- w_uv: bfloat16 [512, 8192], P('rep'), may hold values from -0.25 to 0.25
- w_out: bfloat16 [8192, 7168], P('grp'), may hold values from -0.0625 to 0.0625
- norm_gain: bfloat16 [7168], replicated, may hold values from 0.5 to 1.5
- w_gate: bfloat16 [7168, 18432], P(None, ('rep', 'grp')), may hold values from -0.0625 to 0.0625
- w_up: bfloat16 [7168, 18432], P(None, ('rep', 'grp')), may hold values from -0.0625 to 0.0625
- w_down: bfloat16 [18432, 7168], P(('rep', 'grp')), may hold values from -0.046875 to 0.046875
Outputs:
- hidden_out: bfloat16 [128, 7168], P(('rep', 'grp'))
Inputs may be any that keep to these rules, and one draw needn't show every extreme that they name: `lengths`: every sequence has 2 or more cached positions and at most 4096; some sequence has exactly 4096.
All inputs are finite; a program needn't handle non-finite values.
Results may differ from a plain program's by a relative error of at most 0.03.
Values may be sent and summed in bfloat16 or wider, within the bound.
No kernel may reach another device: no remote copies, remote signals or barrier semaphores. Data moves between devices by JAX's collectives and lax.ppermute only.
A program may use at most 192 MiB of HBM per device.

v0:
```python
import functools

import jax
import jax.numpy as jnp
from jax import lax
from jax.experimental import pallas as pl
from jax.experimental.pallas import tpu as pltpu
from jax.sharding import PartitionSpec as P


NOPE = 128
ROPE = 64
VH = 128

AXES = ("rep", "grp")
epsilon = 1e-06


MIB = 1024 * 1024
IN_HBM = pl.BlockSpec(memory_space=pltpu.HBM)
IN_VMEM = pl.BlockSpec(memory_space=pltpu.VMEM)
IN_SMEM = pl.BlockSpec(memory_space=pltpu.SMEM)
NT = (((1,), (1,)), ((), ()))


def chunk_of(size, wanted):
    chunk = wanted
    while size % chunk:
        chunk //= 2
    return chunk


def attend_kernel(lengths, place, group, *refs, chunk, scale, whole):
    pieces = refs[: place.shape[0]]
    (
        q_rope, new_kv, cache_hbm, weight_hbm, near, far, weight, cache, queries, scores, total,
        sems, weight_sems,
    ) = refs[place.shape[0] :]
    weight_rows = weight.shape[0] // weight_sems.shape[0]
    weight_copies = [
        pltpu.make_async_copy(
            weight_hbm.at[pl.ds(i * weight_rows, weight_rows)],
            weight.at[pl.ds(i * weight_rows, weight_rows)],
            weight_sems.at[i],
        )
        for i in range(weight_sems.shape[0])
    ]
    seqs, heads, own_rank = pieces[0].shape
    rank = own_rank * len(pieces)

    def part(i):
        return pl.ds(pl.multiple_of(i * chunk, chunk), chunk)

    def used(b):
        return (lengths[b] + (chunk - 1)) // chunk

    def copy(b, i):
        return pltpu.make_async_copy(
            cache_hbm.at[b, :, part(i)], cache.at[b, :, part(i)], sems.at[b, i]
        )

    for b in range(seqs):

        @pl.loop(0, used(b))
        def _(i):
            copy(b, i).start()

    for weight_copy in weight_copies:
        weight_copy.start()

    for b in range(seqs):
        for j, piece in enumerate(pieces):
            columns = pl.ds(pl.multiple_of(place[j] * own_rank, own_rank), own_rank)
            queries[b, :, columns] = piece[b]
        queries[b, :, rank:] = q_rope[b]

    steps = used(0)
    for b in range(1, seqs):
        steps = steps + used(b)
    copy(0, 0).wait()
    scores[0] = jnp.dot(queries[0], cache[0, :, part(0)], preferred_element_type=jnp.float32)

    def step(t, carry):
        b, i, top, denom = carry
        slot = t & 1
        last = i + 1 == used(b)
        next_b = jnp.where(last, b + 1, b)
        next_i = jnp.where(last, 0, i + 1)

        @pl.when(t + 1 < steps)
        def _():
            copy(next_b, next_i).wait()

        ahead_b = jnp.minimum(next_b, seqs - 1)
        first = i == 0
        own = new_kv[b].astype(jnp.float32)
        own_score = jnp.sum(queries[b].astype(jnp.float32) * own, axis=1, keepdims=True)
        top = jnp.where(first, own_score, top)
        denom = jnp.where(first, 1.0, denom)
        ahead = jnp.dot(
            queries[ahead_b], cache[ahead_b, :, part(next_i)], preferred_element_type=jnp.float32
        )
        position = i * chunk + lax.broadcasted_iota(jnp.int32, (1, chunk), 1)
        raw = scores[slot] + jnp.where(position < lengths[b], 0.0, -jnp.inf)
        new_top = jnp.maximum(top, jnp.max(raw, axis=1, keepdims=True))
        weights = jnp.exp((raw - new_top) * scale)
        shrink = jnp.exp((top - new_top) * scale)
        denom = denom * shrink + jnp.sum(weights, axis=1, keepdims=True)
        before = jnp.where(first, jnp.broadcast_to(own[:, :rank], (heads, rank)), total[...])
        fresh = before * shrink + lax.dot_general(
            weights.astype(jnp.bfloat16),
            cache[b, :rank, part(i)],
            NT,
            preferred_element_type=jnp.float32,
        )
        scores[1 - slot] = ahead
        total[...] = fresh

        @pl.when(last)
        def _():
            if whole:
                near[b] = (fresh / denom).astype(near.dtype)
                return
            total[...] = fresh / denom
            own_heads = heads // (2 * near.shape[0])
            place_rows = pl.ds(pl.multiple_of(b * own_heads, own_heads), own_heads)
            for x, block in enumerate((near, far)):
                for high in range(near.shape[0]):
                    first_head = (group[0] ^ (2 * high + x)) * own_heads
                    rows = pl.ds(pl.multiple_of(first_head, own_heads), own_heads)
                    block[high, place_rows, :] = total[rows, :].astype(block.dtype)

        return next_b, next_i, new_top, denom

    zero = jnp.zeros((heads, 1), jnp.float32)
    lax.fori_loop(0, steps, step, (jnp.int32(0), jnp.int32(0), zero, zero))
    for weight_copy in weight_copies:
        weight_copy.wait()


def attend(
    lengths, place, group, pieces, q_rope, new_kv, cache_kv, w_out, scale, grp_size
):
    seqs, heads, own_rank = pieces[0].shape
    rank = own_rank * len(pieces)
    capacity, depth = cache_kv.shape[1:]
    chunk = chunk_of(capacity, 1024)
    own_heads = heads // grp_size
    whole = own_heads % 8 != 0
    shapes = [(grp_size // 2, seqs * own_heads, rank)] * 2
    if whole:
        shapes = [(seqs, heads, rank), (8, 128)]
    blocks = [jax.ShapeDtypeStruct(shape, jnp.bfloat16) for shape in shapes]
    near, far, out_weight = pl.pallas_call(
        functools.partial(attend_kernel, chunk=chunk, scale=scale, whole=whole),
        out_shape=(*blocks, jax.ShapeDtypeStruct(w_out.shape, w_out.dtype)),
        in_specs=[IN_SMEM] * 3 + [IN_VMEM] * (len(pieces) + 2) + [IN_HBM] * 2,
        out_specs=(IN_VMEM,) * 3,
        scratch_shapes=[
            pltpu.VMEM((seqs, depth, capacity), jnp.bfloat16),
            pltpu.VMEM((seqs, heads, depth), jnp.bfloat16),
            pltpu.VMEM((2, heads, chunk), jnp.float32),
            pltpu.VMEM((heads, rank), jnp.float32),
            pltpu.SemaphoreType.DMA((seqs, capacity // chunk)),
            pltpu.SemaphoreType.DMA((4,)),
        ],
        compiler_params=pltpu.CompilerParams(vmem_limit_bytes=30 * MIB),
        cost_estimate=pl.CostEstimate(
            flops=4 * seqs * heads * capacity * depth,
            bytes_accessed=2 * seqs * capacity * depth,
            transcendentals=seqs * heads * capacity,
        ),
        name="attend",
    )(lengths, place, group, *pieces, q_rope, new_kv[:, None, :], cache_kv.transpose(0, 2, 1), w_out)
    if whole:
        latent = near.reshape(seqs, grp_size, own_heads, rank).swapaxes(0, 1)
        latent = latent.reshape(grp_size, seqs * own_heads, rank)
        latent = jnp.take(latent, group[0] ^ jnp.arange(grp_size), axis=0)
        near, far = latent[0::2], latent[1::2]
    return near, far, out_weight


def slice_kernel(start, source, out, sem):
    width = out.shape[1]
    columns = pl.ds(pl.multiple_of(start[0] * width, width), width)
    copy = pltpu.make_async_copy(source.at[:, columns], out, sem)
    copy.start()
    copy.wait()


def own_columns(source, index, width):
    return pl.pallas_call(
        slice_kernel,
        out_shape=jax.ShapeDtypeStruct((source.shape[0], width), source.dtype),
        in_specs=[IN_SMEM, IN_HBM],
        out_specs=IN_VMEM,
        scratch_shapes=[pltpu.SemaphoreType.DMA(())],
        cost_estimate=pl.CostEstimate(flops=0, bytes_accessed=4 * source.shape[0] * width, transcendentals=0),
        name="own_columns",
    )(index.reshape(1), source)


def out_kernel(place, *refs, chunk, seqs, blocks_of):
    pieces = refs[: place.shape[0]]
    latents = refs[place.shape[0] : place.shape[0] + len(blocks_of)]
    weight, keep, send, value, every, heads_in = refs[place.shape[0] + len(blocks_of) :]
    own_rank = pieces[0].shape[0]
    for j, piece in enumerate(pieces):
        rows = pl.ds(pl.multiple_of(place[j] * own_rank, own_rank), own_rank)
        value[rows, :] = piece[...]
    own_heads = every.shape[0]
    for latent, blocks in zip(latents, blocks_of):
        count = latent.shape[0]
        product = jnp.dot(latent[...], value[...], preferred_element_type=jnp.float32)
        for h in range(own_heads):
            columns = slice(h * VH, (h + 1) * VH)
            every[h, :count, :] = product[:, columns]
            for i, block in enumerate(blocks):
                heads_in[block * seqs : (block + 1) * seqs, columns] = every[
                    h, pl.ds(i * seqs * own_heads + h, seqs, own_heads), :
                ]
    rows_in = heads_in[...].astype(jnp.bfloat16)
    half = keep.shape[0]

    @pl.loop(0, keep.shape[1] // chunk)
    def _(i):
        part = pl.ds(pl.multiple_of(i * chunk, chunk), chunk)
        result = jnp.dot(rows_in, weight[:, part], preferred_element_type=jnp.float32)
        keep[:, part] = result[:half]
        send[:, part] = result[half:].astype(send.dtype)


def out_proj(place, pieces, latents, blocks_of, w_out, seqs):
    depth, width = w_out.shape
    rank = latents[0].shape[1]
    rows = seqs * sum(len(blocks) for blocks in blocks_of)
    return pl.pallas_call(
        functools.partial(
            out_kernel, chunk=chunk_of(width, 3584), seqs=seqs, blocks_of=blocks_of
        ),
        out_shape=(
            jax.ShapeDtypeStruct((rows // 2, width), jnp.float32),
            jax.ShapeDtypeStruct((rows // 2, width), jnp.bfloat16),
        ),
        in_specs=[IN_SMEM] + [IN_VMEM] * (len(pieces) + len(latents) + 1),
        out_specs=(IN_VMEM, IN_VMEM),
        scratch_shapes=[
            pltpu.VMEM((rank, depth), jnp.bfloat16),
            pltpu.VMEM((depth // VH, latents[0].shape[0], VH), jnp.float32),
            pltpu.VMEM((rows, depth), jnp.float32),
        ],
        compiler_params=pltpu.CompilerParams(vmem_limit_bytes=12 * MIB),
        cost_estimate=pl.CostEstimate(
            flops=2 * rows * width * depth,
            bytes_accessed=2 * depth * width,
            transcendentals=0,
        ),
        name="out_proj",
    )(place, *pieces, *latents, w_out)


def mlp_kernel(
    own_low, own_high, other_low, other_high, gate, up_hbm, down_hbm,
    keep_low, keep_high, send,
    up, down, gate_sum, up_sum, active, sems, *, chunk
):
    half, middle = own_low.shape
    count = middle // chunk

    def part(i):
        return pl.ds(pl.multiple_of(i * chunk, chunk), chunk)

    def up_copy(i):
        return pltpu.make_async_copy(up_hbm.at[:, part(i)], up.at[:, part(i)], sems.at[0, i])

    def down_copy(i):
        return pltpu.make_async_copy(down_hbm.at[:, part(i)], down.at[:, part(i)], sems.at[1, i])

    @pl.loop(0, 2 * count)
    def _(i):
        up_copy(i).start()

    @pl.loop(0, 2 * count)
    def _(i):
        down_copy(i).start()

    sides = ((own_low, other_low), (own_high, other_high))
    for weight, total in ((gate, gate_sum), (up, up_sum)):
        total[...] = jnp.zeros_like(total)
        for side, (own, other) in enumerate(sides):

            @pl.loop(0, count)
            def _(i):
                rows = jnp.concatenate([own[:, part(i)], other[:, part(i)]], axis=0)
                if weight is up:
                    up_copy(i + side * count).wait()
                total[...] += lax.dot_general(
                    weight[:, part(i + side * count)],
                    rows,
                    NT,
                    preferred_element_type=jnp.float32,
                )

    value = gate_sum[...]
    active[...] = (value / (1.0 + jnp.exp(-value)) * up_sum[...]).T.astype(jnp.bfloat16)
    for side, keep in enumerate((keep_low, keep_high)):

        @pl.loop(0, count)
        def _(i):
            down_copy(i + side * count).wait()
            columns = part(i + side * count)
            result = jnp.dot(active[...], down[:, columns], preferred_element_type=jnp.float32)
            keep[:, part(i)] = result[:half].astype(keep.dtype)
            send[:, columns] = result[half:].astype(send.dtype)


def gated_mlp(own, other, gate_rows, up_rows, w_down):
    half, middle = own[0].shape
    hidden, width = w_down.shape
    return pl.pallas_call(
        functools.partial(mlp_kernel, chunk=chunk_of(middle, 1792)),
        out_shape=(
            jax.ShapeDtypeStruct((half, middle), jnp.float32),
            jax.ShapeDtypeStruct((half, middle), jnp.float32),
            jax.ShapeDtypeStruct((half, width), jnp.bfloat16),
        ),
        in_specs=[IN_VMEM] * 5 + [IN_HBM] * 2,
        out_specs=(IN_VMEM,) * 3,
        scratch_shapes=[
            pltpu.VMEM((hidden, width), jnp.bfloat16),
            pltpu.VMEM((hidden, width), jnp.bfloat16),
            pltpu.VMEM((hidden, 2 * half), jnp.float32),
            pltpu.VMEM((hidden, 2 * half), jnp.float32),
            pltpu.VMEM((2 * half, hidden), jnp.bfloat16),
            pltpu.SemaphoreType.DMA((2, width // chunk_of(middle, 1792))),
        ],
        compiler_params=pltpu.CompilerParams(vmem_limit_bytes=38 * MIB),
        cost_estimate=pl.CostEstimate(
            flops=12 * half * width * hidden,
            bytes_accessed=6 * hidden * width,
            transcendentals=2 * half * hidden,
        ),
        name="gated_mlp",
    )(*own, *other, gate_rows, up_rows, w_down)


def direct_phases(rep_size, grp_size):
    out = []
    for axis, size, low in (("grp", grp_size, 2), ("rep", rep_size, 4)):
        bit = size
        while bit > low:
            ways = 4 if bit // 4 >= low else 2
            bit //= ways
            out.append((axis, size, bit, ways))
    return out


def gather_rows(rows, move, sizes):
    held = rows
    for axis, size, bit, ways in direct_phases(*sizes):
        held = jnp.concatenate([held] + [move(held, axis, bit * k) for k in range(1, ways)], axis=0)
    n, width = held.shape
    low, high = held[:, : width // 2], held[:, width // 2 :]
    low_x, high_y = move(low, "grp", 1), move(high, "rep", 2)
    low = jnp.concatenate([low, low_x], axis=0)
    wide = jnp.concatenate([high, high_y], axis=0)
    low_y, high_x = move(low, "rep", 2), move(wide, "grp", 1)
    low = jnp.concatenate([low, low_y], axis=0)
    high = jnp.concatenate([high, high_x[:n], high_y, high_x[n:]], axis=0)
    return (low, high), (move(low, "rep", 1), move(high, "rep", 1))


def scatter_sum(low, high, send, move, sizes):
    def add(mine, theirs):
        return mine + theirs.astype(jnp.float32)

    def narrow(value):
        return value.astype(jnp.bfloat16)

    middle = low.shape[1]
    n = low.shape[0] // 4
    got = move(send, "rep", 1)
    low, high = add(low, got[:, :middle]), add(high, got[:, middle:])
    low_got = move(narrow(low[2 * n :]), "rep", 2)
    high_got = move(narrow(jnp.concatenate([high[n : 2 * n], high[3 * n :]], axis=0)), "grp", 1)
    low = add(low[: 2 * n], low_got)
    high = add(jnp.concatenate([high[:n], high[2 * n : 3 * n]], axis=0), high_got)
    low_got, high_got = move(narrow(low[n:]), "grp", 1), move(narrow(high[n:]), "rep", 2)
    total = jnp.concatenate([add(low[:n], low_got), add(high[:n], high_got)], axis=1)
    for axis, size, bit, ways in reversed(direct_phases(*sizes)):
        per = total.shape[0] // ways
        moved = [
            move(narrow(total[k * per : (k + 1) * per]), axis, bit * k) for k in range(1, ways)
        ]
        total = total[:per]
        for piece in moved:
            total = add(total, piece)
    return total


def to_heads(near, far, move, sizes):
    got = move(far, "grp", 1)
    order = [phase for phase in direct_phases(*sizes) if phase[0] == "grp"]
    high = near.shape[0]
    held, senders = jnp.stack([near, got], axis=1), [0, high]
    if not order:
        return [held.reshape(-1, held.shape[-1])], (tuple(senders),)
    for n, (axis, size, bit, ways) in enumerate(order):
        per = held.shape[0] // ways
        weight = per
        parts = [held[k * per : (k + 1) * per] for k in range(ways)]
        parts = parts[:1] + [move(parts[k], axis, bit * k) for k in range(1, ways)]
        named = [[sender + k * weight for sender in senders] for k in range(ways)]
        if n + 1 < len(order):
            held, senders = jnp.concatenate(parts, axis=1), sum(named, [])
    return (
        [part.reshape(-1, part.shape[-1]) for part in parts],
        tuple(tuple(names) for names in named),
    )


def sum_heads(keep, send, move, sizes):
    got = move(send, "grp", 1)
    total = keep + got.astype(jnp.float32)
    for axis, size, bit, ways in [p for p in direct_phases(*sizes) if p[0] == "grp"]:
        per = total.shape[0] // ways
        moved = [
            move(total[k * per : (k + 1) * per].astype(jnp.bfloat16), axis, bit * k)
            for k in range(1, ways)
        ]
        total = total[:per]
        for piece in moved:
            total = total + piece.astype(jnp.float32)
    return total


def on_device(
    hidden_in,
    q_nope,
    q_rope,
    new_kv,
    cache_kv,
    lengths,
    w_uk,
    w_uv,
    w_out,
    norm_gain,
    w_gate,
    w_up,
    w_down,
    *,
    rep_size,
    grp_size,
):
    sizes = {"rep": rep_size, "grp": grp_size}

    def move(value, axis, bit):
        return lax.ppermute(value, axis, [(i, i ^ bit) for i in range(sizes[axis])])

    seqs, _ = hidden_in.shape
    heads = q_nope.shape[1] // NOPE
    rank_own = w_uk.shape[0]
    own_heads = heads // grp_size

    held = [q_nope]
    for step in range(1, rep_size):
        held.append(move(q_nope, "rep", step))
    held = jnp.concatenate(held, axis=0)
    q_part = jnp.einsum(
        "bhd,chd->bhc",
        held.reshape(seqs * rep_size, heads, NOPE),
        w_uk.reshape(rank_own, heads, NOPE),
        preferred_element_type=jnp.float32,
    ).astype(jnp.bfloat16)
    pieces = []
    for step in range(rep_size):
        piece = q_part[step * seqs : (step + 1) * seqs]
        pieces.append(move(piece, "rep", step) if step else piece)
    place = lax.axis_index("rep") ^ jnp.arange(rep_size, dtype=jnp.int32)

    values = [own_columns(w_uv, lax.axis_index("grp"), own_heads * VH)]
    for step in range(1, rep_size):
        low = step & -step
        values.append(move(values[step ^ low], "rep", low))

    near, far, out_weight = attend(
        lengths,
        place,
        lax.axis_index("grp").reshape(1),
        pieces,
        q_rope.reshape(seqs, heads, ROPE),
        new_kv,
        cache_kv,
        w_out,
        float(NOPE + ROPE) ** (-0.5),
        grp_size,
    )
    latents, blocks_of = to_heads(near, far, move, (rep_size, grp_size))
    keep, send = out_proj(place, values, latents, blocks_of, out_weight, seqs)
    attn_out = sum_heads(keep, send, move, (rep_size, grp_size))
    resid = (hidden_in.astype(jnp.float32) + attn_out).astype(jnp.bfloat16)
    resid_f32 = resid.astype(jnp.float32)
    mean_sq = jnp.mean(resid_f32 * resid_f32, axis=1, keepdims=True)
    normed = (
        resid_f32 * lax.rsqrt(mean_sq + epsilon) * norm_gain.astype(jnp.float32)
    ).astype(jnp.bfloat16)

    own, other = gather_rows(normed, move, (rep_size, grp_size))
    low, high, send = gated_mlp(own, other, w_gate.T, w_up.T, w_down)
    mlp_out = scatter_sum(low, high, send, move, (rep_size, grp_size))
    return (resid_f32 + mlp_out).astype(jnp.bfloat16)


def solution(mesh):
    def body(*args):
        return on_device(*args, rep_size=mesh.shape["rep"], grp_size=mesh.shape["grp"])

    return jax.shard_map(
        body,
        mesh=mesh,
        in_specs=(
            P(AXES, None),
            P(AXES, None),
            P(AXES, None),
            P(AXES, None),
            P(AXES, None, None),
            P(AXES),
            P("rep", None),
            P("rep", None),
            P("grp", None),
            P(),
            P(None, AXES),
            P(None, AXES),
            P(AXES, None),
        ),
        out_specs=P(AXES, None),
        check_vma=False,
    )
```

profile of v0, /device:TPU:0, one launch (start us, length us, event | category | flops | bytes accessed | tf_op | source)
XLA Modules:
  0.0 121.7 jit_solution(16331187033214274071)
XLA Ops:
  0.6 2.6 %collective-permute-start.4 = (bf16[4,8192]{1,0:T(4,128)(2,1)}, bf16[4,8192]{1,0:T(4,128)(2,1)S(1)}, u32[]{:S(2)}, u32[]{:S(2)}) collective-permute-start(bf16[4,8192]{1,0:T(4,128)(2,1)} %param.14), channel_id=1, source_target_pairs={{0,16},{8,24},{16,0},{24,8},{1,17},{9,25},{17,1},{25,9},{2,18},{10... | collective-permute-start | bytes 196616 | tf_op jit(solution)/shard_map/ppermute | solution.py:458
  3.2 1.7 %own_columns.1.refs_0_ = bf16[128,1024]{1,0:T(8,128)(2,1)} custom-call(s32[1]{0:T(128)} %bitcast.start.group, bf16[128,8192]{1,0:T(8,128)(2,1)} %source.1), custom_call_target="tpu_custom_call" | custom-call | bytes 524288 | tf_op jit(solution)/shard_map/own_columns/pallas_call | solution.py:192
  4.9 1.8 %collective-permute-start.1 = (bf16[128,1024]{1,0:T(8,128)(2,1)}, bf16[128,1024]{1,0:T(8,128)(2,1)S(1)}, u32[]{:S(2)}, u32[]{:S(2)}) collective-permute-start(bf16[128,1024]{1,0:T(8,128)(2,1)} %own_columns.1.refs_0_), channel_id=1, source_target_pairs={{0,16},{8,24},{16,0},{24,8},{1,17},{9,25},{17,1},{25,9},{2,18},{10... | collective-permute-start | bytes 786440 | tf_op jit(solution)/shard_map/ppermute | solution.py:458
  9.0 1.4 %collective-permute-start.7 = (bf16[4,64,128]{2,1,0:T(8,128)(2,1)S(1)}, bf16[4,64,128]{2,1,0:T(8,128)(2,1)S(1)}, u32[]{:S(2)}, u32[]{:S(2)}) collective-permute-start(bf16[4,64,128]{2,1,0:T(8,128)(2,1)S(1)} %get-tuple-element.37), channel_id=1, source_target_pairs={{0,16},{8,24},{16,0},{24,8},{1,17},{9,25},{17,1},{25,9},{2,18},{10... | collective-permute-start | bytes 196616 | tf_op jit(solution)/shard_map/ppermute | solution.py:458
  10.7 5.0 %collective-permute-done.7.refs_2_ = bf16[4,64,128]{2,1,0:T(8,128)(2,1)S(1)} collective-permute-done((bf16[4,64,128]{2,1,0:T(8,128)(2,1)S(1)}, bf16[4,64,128]{2,1,0:T(8,128)(2,1)S(1)}, u32[]{:S(2)}, u32[]{:S(2)}) %collective-permute-start.7) | collective-permute-done | bytes 65568 | tf_op jit(solution)/shard_map/ppermute | solution.py:458
  15.9 12.0 %attend.1 = (bf16[4,32,512]{2,1,0:T(8,128)(2,1)S(1)}, bf16[4,32,512]{2,1,0:T(8,128)(2,1)S(1)}, bf16[1024,7168]{1,0:T(8,128)(2,1)S(1)}) custom-call(s32[4]{0:T(128)S(1)} %copy-done.3, s32[4]{0:T(128)S(1)} %iota_xor_fusion.place, s32[1]{0:T(128)} %bitcast.start.group, bf16[4,64,128]{2,1,0:T(8,128)(2,1)S(1)} %get-tuple-element.39.refs_0_, ...), custom_call_target="tpu_custom_call" | custom-call | flops 2415919104 | bytes 18874368 | tf_op jit(solution)/shard_map/attend/pallas_call | solution.py:154
  28.6 4.4 %collective-permute-done.9 = bf16[4,32,512]{2,1,0:T(8,128)(2,1)S(1)} collective-permute-done((bf16[4,32,512]{2,1,0:T(8,128)(2,1)S(1)}, bf16[4,32,512]{2,1,0:T(8,128)(2,1)S(1)}, u32[]{:S(2)}, u32[]{:S(2)}) %collective-permute-start.9) | collective-permute-done | bytes 131104 | tf_op jit(solution)/shard_map/ppermute | solution.py:458
  35.4 2.0 %collective-permute-start.12 = (bf16[1,2,32,512]{3,2,0,1:T(8,128)(2,1)S(1)}, bf16[1,2,32,512]{3,2,0,1:T(8,128)(2,1)S(1)}, u32[]{:S(2)}, u32[]{:S(2)}) collective-permute-start(bf16[1,2,32,512]{3,2,0,1:T(8,128)(2,1)S(1)} %get-tuple-element.32), channel_id=1, source_target_pairs={{0,6},{1,7},{2,4},{3,5},{4,2},{5,3},{6,0},{7,1},{8,14},{9,15},{10,... | collective-permute-start | bytes 196616 | tf_op jit(solution)/shard_map/ppermute | solution.py:458
  38.0 4.2 %collective-permute-done.11 = bf16[1,2,32,512]{3,2,0,1:T(8,128)(2,1)S(1)} collective-permute-done((bf16[1,2,32,512]{3,2,0,1:T(8,128)(2,1)S(1)}, bf16[1,2,32,512]{3,2,0,1:T(8,128)(2,1)S(1)}, u32[]{:S(2)}, u32[]{:S(2)}) %collective-permute-start.11) | collective-permute-done | bytes 65568 | tf_op jit(solution)/shard_map/ppermute | solution.py:458
  42.3 4.2 %out_proj.1 = (f32[16,7168]{1,0:T(8,128)S(1)}, bf16[16,7168]{1,0:T(8,128)(2,1)S(1)}) custom-call(s32[4]{0:T(128)S(1)} %iota_xor_fusion.place, bf16[128,1024]{1,0:T(8,128)(2,1)S(1)} %copy-done.2, bf16[128,1024]{1,0:T(8,128)(2,1)S(1)} %collective-permute-done.refs_1_, bf16[128,1024]{1,0:T(8,128)(2,1)S(1)} %collective-permute-done.1.refs_2_, ...), custom_call_target="tpu_custom_call" | custom-call | flops 469762048 | bytes 14680064 | tf_op jit(solution)/shard_map/out_proj/pallas_call | solution.py:237
  46.8 6.6 %collective-permute-done.13 = bf16[16,7168]{1,0:T(8,128)(2,1)S(1)} collective-permute-done((bf16[16,7168]{1,0:T(8,128)(2,1)S(1)}, bf16[16,7168]{1,0:T(8,128)(2,1)S(1)}, u32[]{:S(2)}, u32[]{:S(2)}) %collective-permute-start.13) | collective-permute-done | bytes 229408 | tf_op jit(solution)/shard_map/ppermute | solution.py:458
  53.6 2.4 %collective-permute-start.14 = (bf16[4,7168]{1,0:T(4,128)(2,1)S(1)}, bf16[4,7168]{1,0:T(4,128)(2,1)S(1)}, u32[]{:S(2)}, u32[]{:S(2)}) collective-permute-start(bf16[4,7168]{1,0:T(4,128)(2,1)S(1)} %get-tuple-element.47), channel_id=1, source_target_pairs={{0,2},{1,3},{2,0},{3,1},{4,6},{5,7},{6,4},{7,5},{8,10},{9,11},{10,... | collective-permute-start | bytes 172040 | tf_op jit(solution)/shard_map/ppermute | solution.py:458
  57.0 1.4 %collective-permute-start.16 = (bf16[4,7168]{1,0:T(4,128)(2,1)S(1)}, bf16[4,7168]{1,0:T(4,128)(2,1)S(1)}, u32[]{:S(2)}, u32[]{:S(2)}) collective-permute-start(bf16[4,7168]{1,0:T(4,128)(2,1)S(1)} %get-tuple-element.48), channel_id=1, source_target_pairs={{0,6},{1,7},{2,4},{3,5},{4,2},{5,3},{6,0},{7,1},{8,14},{9,15},{10,... | collective-permute-start | bytes 172040 | tf_op jit(solution)/shard_map/ppermute | solution.py:458
  58.4 3.7 %collective-permute-done.15 = bf16[4,7168]{1,0:T(4,128)(2,1)S(1)} collective-permute-done((bf16[4,7168]{1,0:T(4,128)(2,1)S(1)}, bf16[4,7168]{1,0:T(4,128)(2,1)S(1)}, u32[]{:S(2)}, u32[]{:S(2)}) %collective-permute-start.15) | collective-permute-done | bytes 57376 | tf_op jit(solution)/shard_map/ppermute | solution.py:458
  64.3 1.8 %collective-permute-start.18 = (bf16[4,7168]{1,0:T(4,128)(2,1)S(1)}, bf16[4,7168]{1,0:T(4,128)(2,1)S(1)}, u32[]{:S(2)}, u32[]{:S(2)}) collective-permute-start(bf16[4,7168]{1,0:T(4,128)(2,1)S(1)} %fusion.9), channel_id=1, source_target_pairs={{0,4},{1,5},{2,6},{3,7},{4,0},{5,1},{6,2},{7,3},{8,12},{9,13},{10,... | collective-permute-start | bytes 172040 | tf_op jit(solution)/shard_map/ppermute | solution.py:458
  66.1 1.8 %collective-permute-start.19 = (bf16[4,7168]{1,0:T(4,128)(2,1)S(1)}, bf16[4,7168]{1,0:T(4,128)(2,1)S(1)}, u32[]{:S(2)}, u32[]{:S(2)}) collective-permute-start(bf16[4,7168]{1,0:T(4,128)(2,1)S(1)} %fusion.9), channel_id=1, source_target_pairs={{0,6},{1,7},{2,4},{3,5},{4,2},{5,3},{6,0},{7,1},{8,14},{9,15},{10,... | collective-permute-start | bytes 172040 | tf_op jit(solution)/shard_map/ppermute | solution.py:458
  67.9 2.5 %collective-permute-done.18 = bf16[4,7168]{1,0:T(4,128)(2,1)S(1)} collective-permute-done((bf16[4,7168]{1,0:T(4,128)(2,1)S(1)}, bf16[4,7168]{1,0:T(4,128)(2,1)S(1)}, u32[]{:S(2)}, u32[]{:S(2)}) %collective-permute-start.18) | collective-permute-done | bytes 57376 | tf_op jit(solution)/shard_map/ppermute | solution.py:458
  70.4 1.7 %collective-permute-done.19 = bf16[4,7168]{1,0:T(4,128)(2,1)S(1)} collective-permute-done((bf16[4,7168]{1,0:T(4,128)(2,1)S(1)}, bf16[4,7168]{1,0:T(4,128)(2,1)S(1)}, u32[]{:S(2)}, u32[]{:S(2)}) %collective-permute-start.19) | collective-permute-done | bytes 57376 | tf_op jit(solution)/shard_map/ppermute | solution.py:458
  74.4 2.7 %collective-permute-done.22 = bf16[16,3584]{1,0:T(8,128)(2,1)S(1)} collective-permute-done((bf16[16,3584]{1,0:T(8,128)(2,1)S(1)}, bf16[16,3584]{1,0:T(8,128)(2,1)S(1)}, u32[]{:S(2)}, u32[]{:S(2)}) %collective-permute-start.22) | collective-permute-done | bytes 114720 | tf_op jit(solution)/shard_map/ppermute | solution.py:458
  80.5 2.8 %collective-permute-done.23 = bf16[32,3584]{1,0:T(8,128)(2,1)S(1)} collective-permute-done((bf16[32,3584]{1,0:T(8,128)(2,1)S(1)}, bf16[32,3584]{1,0:T(8,128)(2,1)S(1)}, u32[]{:S(2)}, u32[]{:S(2)}) %collective-permute-start.23) | collective-permute-done | bytes 229408 | tf_op jit(solution)/shard_map/ppermute | solution.py:458
  83.4 1.8 %collective-permute-done.21 = bf16[32,3584]{1,0:T(8,128)(2,1)S(1)} collective-permute-done((bf16[32,3584]{1,0:T(8,128)(2,1)S(1)}, bf16[32,3584]{1,0:T(8,128)(2,1)S(1)}, u32[]{:S(2)}, u32[]{:S(2)}) %collective-permute-start.21) | collective-permute-done | bytes 229408 | tf_op jit(solution)/shard_map/ppermute | solution.py:458
  85.3 1.8 %collective-permute-done.24.other_low = bf16[64,3584]{1,0:T(8,128)(2,1)S(1)} collective-permute-done((bf16[64,3584]{1,0:T(8,128)(2,1)S(1)}, bf16[64,3584]{1,0:T(8,128)(2,1)S(1)}, u32[]{:S(2)}, u32[]{:S(2)}) %collective-permute-start.24) | collective-permute-done | bytes 458784 | tf_op jit(solution)/shard_map/ppermute | solution.py:458
  87.1 8.2 %gated_mlp.1 = (f32[64,3584]{1,0:T(8,128)S(1)}, f32[64,3584]{1,0:T(8,128)S(1)}, bf16[64,7168]{1,0:T(8,128)(2,1)S(1)}) custom-call(bf16[64,3584]{1,0:T(8,128)(2,1)S(1)} %pad_maximum_fusion.1.own_low, bf16[64,3584]{1,0:T(8,128)(2,1)S(1)} %pad_maximum_fusion.2.own_high, bf16[64,3584]{1,0:T(8,128)(2,1)S(1)} %collective-permute-done.24.other_low, ...), custom_call_target="tpu_custom_call" | custom-call | flops 3170893824 | bytes 24772608 | tf_op jit(solution)/shard_map/gated_mlp/pallas_call | solution.py:320
  95.6 2.4 %collective-permute-done.26 = bf16[64,7168]{1,0:T(8,128)(2,1)S(1)} collective-permute-done((bf16[64,7168]{1,0:T(8,128)(2,1)S(1)}, bf16[64,7168]{1,0:T(8,128)(2,1)S(1)}, u32[]{:S(2)}, u32[]{:S(2)}) %collective-permute-start.26) | collective-permute-done | bytes 917536 | tf_op jit(solution)/shard_map/ppermute | solution.py:458
  98.2 1.4 %collective-permute-start.29 = (bf16[32,3584]{1,0:T(8,128)(2,1)S(1)}, bf16[32,3584]{1,0:T(8,128)(2,1)S(1)}, u32[]{:S(2)}, u32[]{:S(2)}) collective-permute-start(bf16[32,3584]{1,0:T(8,128)(2,1)S(1)} %pad_maximum_fusion.6), channel_id=1, source_target_pairs={{0,1},{1,0},{2,3},{3,2},{4,5},{5,4},{6,7},{7,6},{8,9},{9,8},{10,11... | collective-permute-start | bytes 688136 | tf_op jit(solution)/shard_map/ppermute | solution.py:458
  100.4 5.5 %collective-permute-done.29 = bf16[32,3584]{1,0:T(8,128)(2,1)S(1)} collective-permute-done((bf16[32,3584]{1,0:T(8,128)(2,1)S(1)}, bf16[32,3584]{1,0:T(8,128)(2,1)S(1)}, u32[]{:S(2)}, u32[]{:S(2)}) %collective-permute-start.29) | collective-permute-done | bytes 229408 | tf_op jit(solution)/shard_map/ppermute | solution.py:458
  108.2 2.6 %collective-permute-done.30 = bf16[16,3584]{1,0:T(8,128)(2,1)S(1)} collective-permute-done((bf16[16,3584]{1,0:T(8,128)(2,1)S(1)}, bf16[16,3584]{1,0:T(8,128)(2,1)S(1)}, u32[]{:S(2)}, u32[]{:S(2)}) %collective-permute-start.30) | collective-permute-done | bytes 114720 | tf_op jit(solution)/shard_map/ppermute | solution.py:458
  110.8 1.4 %collective-permute-done.28 = bf16[16,3584]{1,0:T(8,128)(2,1)S(1)} collective-permute-done((bf16[16,3584]{1,0:T(8,128)(2,1)S(1)}, bf16[16,3584]{1,0:T(8,128)(2,1)S(1)}, u32[]{:S(2)}, u32[]{:S(2)}) %collective-permute-start.28) | collective-permute-done | bytes 114720 | tf_op jit(solution)/shard_map/ppermute | solution.py:458
  112.5 2.6 %collective-permute-start.32 = (bf16[4,7168]{1,0:T(4,128)(2,1)S(1)}, bf16[4,7168]{1,0:T(4,128)(2,1)S(1)}, u32[]{:S(2)}, u32[]{:S(2)}) collective-permute-start(bf16[4,7168]{1,0:T(4,128)(2,1)S(1)} %get-tuple-element.42), channel_id=1, source_target_pairs={{0,4},{1,5},{2,6},{3,7},{4,0},{5,1},{6,2},{7,3},{8,12},{9,13},{10,... | collective-permute-start | bytes 172040 | tf_op jit(solution)/shard_map/ppermute | solution.py:458
  115.1 1.8 %collective-permute-start.33 = (bf16[4,7168]{1,0:T(4,128)(2,1)S(1)}, bf16[4,7168]{1,0:T(4,128)(2,1)S(1)}, u32[]{:S(2)}, u32[]{:S(2)}) collective-permute-start(bf16[4,7168]{1,0:T(4,128)(2,1)S(1)} %get-tuple-element.41), channel_id=1, source_target_pairs={{0,6},{1,7},{2,4},{3,5},{4,2},{5,3},{6,0},{7,1},{8,14},{9,15},{10,... | collective-permute-start | bytes 172040 | tf_op jit(solution)/shard_map/ppermute | solution.py:458
  116.8 1.4 %collective-permute-done.32 = bf16[4,7168]{1,0:T(4,128)(2,1)S(1)} collective-permute-done((bf16[4,7168]{1,0:T(4,128)(2,1)S(1)}, bf16[4,7168]{1,0:T(4,128)(2,1)S(1)}, u32[]{:S(2)}, u32[]{:S(2)}) %collective-permute-start.32) | collective-permute-done | bytes 57376 | tf_op jit(solution)/shard_map/ppermute | solution.py:458
  118.2 2.8 %collective-permute-done.33 = bf16[4,7168]{1,0:T(4,128)(2,1)S(1)} collective-permute-done((bf16[4,7168]{1,0:T(4,128)(2,1)S(1)}, bf16[4,7168]{1,0:T(4,128)(2,1)S(1)}, u32[]{:S(2)}, u32[]{:S(2)}) %collective-permute-start.33) | collective-permute-done | bytes 57376 | tf_op jit(solution)/shard_map/ppermute | solution.py:458
  (97 shorter events, 21.0 us)
Async XLA Ops:
  0.0 6.8 %collective-permute-start.3 = (bf16[4,8192]{1,0:T(4,128)(2,1)}, bf16[4,8192]{1,0:T(4,128)(2,1)S(1)}, u32[]{:S(2)}, u32[]{:S(2)}) collective-permute-start(bf16[4,8192]{1,0:T(4,128)(2,1)} %param.14), channel_id=1, source_target_pairs={{0,8},{8,0},{16,24},{24,16},{1,9},{9,1},{17,25},{25,17},{2,10},{10... | collective-permute-start | bytes 196616 | tf_op jit(solution)/shard_map/ppermute | solution.py:458
  0.6 6.3 %collective-permute-start.4 = (bf16[4,8192]{1,0:T(4,128)(2,1)}, bf16[4,8192]{1,0:T(4,128)(2,1)S(1)}, u32[]{:S(2)}, u32[]{:S(2)}) collective-permute-start(bf16[4,8192]{1,0:T(4,128)(2,1)} %param.14), channel_id=1, source_target_pairs={{0,16},{8,24},{16,0},{24,8},{1,17},{9,25},{17,1},{25,9},{2,18},{10... | collective-permute-start | bytes 196616 | tf_op jit(solution)/shard_map/ppermute | solution.py:458
  3.2 4.3 %collective-permute-start.5 = (bf16[4,8192]{1,0:T(4,128)(2,1)}, bf16[4,8192]{1,0:T(4,128)(2,1)S(1)}, u32[]{:S(2)}, u32[]{:S(2)}) collective-permute-start(bf16[4,8192]{1,0:T(4,128)(2,1)} %param.14), channel_id=1, source_target_pairs={{0,24},{8,16},{16,8},{24,0},{1,25},{9,17},{17,9},{25,1},{2,26},{10... | collective-permute-start | bytes 196616 | tf_op jit(solution)/shard_map/ppermute | solution.py:458
  4.9 23.2 %collective-permute-start.1 = (bf16[128,1024]{1,0:T(8,128)(2,1)}, bf16[128,1024]{1,0:T(8,128)(2,1)S(1)}, u32[]{:S(2)}, u32[]{:S(2)}) collective-permute-start(bf16[128,1024]{1,0:T(8,128)(2,1)} %own_columns.1.refs_0_), channel_id=1, source_target_pairs={{0,16},{8,24},{16,0},{24,8},{1,17},{9,25},{17,1},{25,9},{2,18},{10... | collective-permute-start | bytes 786440 | tf_op jit(solution)/shard_map/ppermute | solution.py:458
  9.0 6.7 %collective-permute-start.7 = (bf16[4,64,128]{2,1,0:T(8,128)(2,1)S(1)}, bf16[4,64,128]{2,1,0:T(8,128)(2,1)S(1)}, u32[]{:S(2)}, u32[]{:S(2)}) collective-permute-start(bf16[4,64,128]{2,1,0:T(8,128)(2,1)S(1)} %get-tuple-element.37), channel_id=1, source_target_pairs={{0,16},{8,24},{16,0},{24,8},{1,17},{9,25},{17,1},{25,9},{2,18},{10... | collective-permute-start | bytes 196616 | tf_op jit(solution)/shard_map/ppermute | solution.py:458
  10.4 5.5 %collective-permute-start.8 = (bf16[4,64,128]{2,1,0:T(8,128)(2,1)S(1)}, bf16[4,64,128]{2,1,0:T(8,128)(2,1)S(1)}, u32[]{:S(2)}, u32[]{:S(2)}) collective-permute-start(bf16[4,64,128]{2,1,0:T(8,128)(2,1)S(1)} %get-tuple-element.36), channel_id=1, source_target_pairs={{0,24},{8,16},{16,8},{24,0},{1,25},{9,17},{17,9},{25,1},{2,26},{10... | collective-permute-start | bytes 196616 | tf_op jit(solution)/shard_map/ppermute | solution.py:458
  27.9 5.0 %collective-permute-start.9 = (bf16[4,32,512]{2,1,0:T(8,128)(2,1)S(1)}, bf16[4,32,512]{2,1,0:T(8,128)(2,1)S(1)}, u32[]{:S(2)}, u32[]{:S(2)}) collective-permute-start(bf16[4,32,512]{2,1,0:T(8,128)(2,1)S(1)} %get-tuple-element.14), channel_id=1, source_target_pairs={{0,1},{1,0},{2,3},{3,2},{4,5},{5,4},{6,7},{7,6},{8,9},{9,8},{10,11... | collective-permute-start | bytes 393224 | tf_op jit(solution)/shard_map/ppermute | solution.py:458
  28.0 9.4 %collective-permute-start = (bf16[128,1024]{1,0:T(8,128)(2,1)S(1)}, bf16[128,1024]{1,0:T(8,128)(2,1)S(1)}, u32[]{:S(2)}, u32[]{:S(2)}) collective-permute-start(bf16[128,1024]{1,0:T(8,128)(2,1)S(1)} %copy-done.2), channel_id=1, source_target_pairs={{0,8},{8,0},{16,24},{24,16},{1,9},{9,1},{17,25},{25,17},{2,10},{10... | collective-permute-start | bytes 786440 | tf_op jit(solution)/shard_map/ppermute | solution.py:458
  28.1 14.2 %collective-permute-start.2 = (bf16[128,1024]{1,0:T(8,128)(2,1)S(1)}, bf16[128,1024]{1,0:T(8,128)(2,1)S(1)}, u32[]{:S(2)}, u32[]{:S(2)}) collective-permute-start(bf16[128,1024]{1,0:T(8,128)(2,1)S(1)} %collective-permute-done.1.refs_2_), channel_id=1, source_target_pairs={{0,8},{8,0},{16,24},{24,16},{1,9},{9,1},{17,25},{25,17},{2,10},{10... | collective-permute-start | bytes 786440 | tf_op jit(solution)/shard_map/ppermute | solution.py:458
  33.0 5.0 %collective-permute-start.10 = (bf16[1,2,32,512]{3,2,0,1:T(8,128)(2,1)S(1)}, bf16[1,2,32,512]{3,2,0,1:T(8,128)(2,1)S(1)}, u32[]{:S(2)}, u32[]{:S(2)}) collective-permute-start(bf16[1,2,32,512]{3,2,0,1:T(8,128)(2,1)S(1)} %get-tuple-element.34), channel_id=1, source_target_pairs={{0,2},{1,3},{2,0},{3,1},{4,6},{5,7},{6,4},{7,5},{8,10},{9,11},{10,... | collective-permute-start | bytes 196616 | tf_op jit(solution)/shard_map/ppermute | solution.py:458
  34.1 8.1 %collective-permute-start.11 = (bf16[1,2,32,512]{3,2,0,1:T(8,128)(2,1)S(1)}, bf16[1,2,32,512]{3,2,0,1:T(8,128)(2,1)S(1)}, u32[]{:S(2)}, u32[]{:S(2)}) collective-permute-start(bf16[1,2,32,512]{3,2,0,1:T(8,128)(2,1)S(1)} %get-tuple-element.35), channel_id=1, source_target_pairs={{0,4},{1,5},{2,6},{3,7},{4,0},{5,1},{6,2},{7,3},{8,12},{9,13},{10,... | collective-permute-start | bytes 196616 | tf_op jit(solution)/shard_map/ppermute | solution.py:458
  35.4 6.8 %collective-permute-start.12 = (bf16[1,2,32,512]{3,2,0,1:T(8,128)(2,1)S(1)}, bf16[1,2,32,512]{3,2,0,1:T(8,128)(2,1)S(1)}, u32[]{:S(2)}, u32[]{:S(2)}) collective-permute-start(bf16[1,2,32,512]{3,2,0,1:T(8,128)(2,1)S(1)} %get-tuple-element.32), channel_id=1, source_target_pairs={{0,6},{1,7},{2,4},{3,5},{4,2},{5,3},{6,0},{7,1},{8,14},{9,15},{10,... | collective-permute-start | bytes 196616 | tf_op jit(solution)/shard_map/ppermute | solution.py:458
  46.5 6.9 %collective-permute-start.13 = (bf16[16,7168]{1,0:T(8,128)(2,1)S(1)}, bf16[16,7168]{1,0:T(8,128)(2,1)S(1)}, u32[]{:S(2)}, u32[]{:S(2)}) collective-permute-start(bf16[16,7168]{1,0:T(8,128)(2,1)S(1)} %get-tuple-element.17), channel_id=1, source_target_pairs={{0,1},{1,0},{2,3},{3,2},{4,5},{5,4},{6,7},{7,6},{8,9},{9,8},{10,11... | collective-permute-start | bytes 688136 | tf_op jit(solution)/shard_map/ppermute | solution.py:458
  53.6 4.8 %collective-permute-start.14 = (bf16[4,7168]{1,0:T(4,128)(2,1)S(1)}, bf16[4,7168]{1,0:T(4,128)(2,1)S(1)}, u32[]{:S(2)}, u32[]{:S(2)}) collective-permute-start(bf16[4,7168]{1,0:T(4,128)(2,1)S(1)} %get-tuple-element.47), channel_id=1, source_target_pairs={{0,2},{1,3},{2,0},{3,1},{4,6},{5,7},{6,4},{7,5},{8,10},{9,11},{10,... | collective-permute-start | bytes 172040 | tf_op jit(solution)/shard_map/ppermute | solution.py:458
  56.0 6.2 %collective-permute-start.15 = (bf16[4,7168]{1,0:T(4,128)(2,1)S(1)}, bf16[4,7168]{1,0:T(4,128)(2,1)S(1)}, u32[]{:S(2)}, u32[]{:S(2)}) collective-permute-start(bf16[4,7168]{1,0:T(4,128)(2,1)S(1)} %get-tuple-element.49), channel_id=1, source_target_pairs={{0,4},{1,5},{2,6},{3,7},{4,0},{5,1},{6,2},{7,3},{8,12},{9,13},{10,... | collective-permute-start | bytes 172040 | tf_op jit(solution)/shard_map/ppermute | solution.py:458
  57.0 6.1 %collective-permute-start.16 = (bf16[4,7168]{1,0:T(4,128)(2,1)S(1)}, bf16[4,7168]{1,0:T(4,128)(2,1)S(1)}, u32[]{:S(2)}, u32[]{:S(2)}) collective-permute-start(bf16[4,7168]{1,0:T(4,128)(2,1)S(1)} %get-tuple-element.48), channel_id=1, source_target_pairs={{0,6},{1,7},{2,4},{3,5},{4,2},{5,3},{6,0},{7,1},{8,14},{9,15},{10,... | collective-permute-start | bytes 172040 | tf_op jit(solution)/shard_map/ppermute | solution.py:458
  63.4 4.5 %collective-permute-start.17 = (bf16[4,7168]{1,0:T(4,128)(2,1)S(1)}, bf16[4,7168]{1,0:T(4,128)(2,1)S(1)}, u32[]{:S(2)}, u32[]{:S(2)}) collective-permute-start(bf16[4,7168]{1,0:T(4,128)(2,1)S(1)} %fusion.9), channel_id=1, source_target_pairs={{0,2},{1,3},{2,0},{3,1},{4,6},{5,7},{6,4},{7,5},{8,10},{9,11},{10,... | collective-permute-start | bytes 172040 | tf_op jit(solution)/shard_map/ppermute | solution.py:458
  64.3 6.1 %collective-permute-start.18 = (bf16[4,7168]{1,0:T(4,128)(2,1)S(1)}, bf16[4,7168]{1,0:T(4,128)(2,1)S(1)}, u32[]{:S(2)}, u32[]{:S(2)}) collective-permute-start(bf16[4,7168]{1,0:T(4,128)(2,1)S(1)} %fusion.9), channel_id=1, source_target_pairs={{0,4},{1,5},{2,6},{3,7},{4,0},{5,1},{6,2},{7,3},{8,12},{9,13},{10,... | collective-permute-start | bytes 172040 | tf_op jit(solution)/shard_map/ppermute | solution.py:458
  66.1 6.0 %collective-permute-start.19 = (bf16[4,7168]{1,0:T(4,128)(2,1)S(1)}, bf16[4,7168]{1,0:T(4,128)(2,1)S(1)}, u32[]{:S(2)}, u32[]{:S(2)}) collective-permute-start(bf16[4,7168]{1,0:T(4,128)(2,1)S(1)} %fusion.9), channel_id=1, source_target_pairs={{0,6},{1,7},{2,4},{3,5},{4,2},{5,3},{6,0},{7,1},{8,14},{9,15},{10,... | collective-permute-start | bytes 172040 | tf_op jit(solution)/shard_map/ppermute | solution.py:458
  72.3 4.9 %collective-permute-start.22 = (bf16[16,3584]{1,0:T(8,128)(2,1)S(1)}, bf16[16,3584]{1,0:T(8,128)(2,1)S(1)}, u32[]{:S(2)}, u32[]{:S(2)}) collective-permute-start(bf16[16,3584]{1,0:T(8,128)(2,1)S(1)} %get-tuple-element.45), channel_id=1, source_target_pairs={{0,16},{8,24},{16,0},{24,8},{1,17},{9,25},{17,1},{25,9},{2,18},{10... | collective-permute-start | bytes 344072 | tf_op jit(solution)/shard_map/ppermute | solution.py:458
  73.1 6.0 %collective-permute-start.20 = (bf16[16,3584]{1,0:T(8,128)(2,1)S(1)}, bf16[16,3584]{1,0:T(8,128)(2,1)S(1)}, u32[]{:S(2)}, u32[]{:S(2)}) collective-permute-start(bf16[16,3584]{1,0:T(8,128)(2,1)S(1)} %get-tuple-element.46), channel_id=1, source_target_pairs={{0,1},{1,0},{2,3},{3,2},{4,5},{5,4},{6,7},{7,6},{8,9},{9,8},{10,11... | collective-permute-start | bytes 344072 | tf_op jit(solution)/shard_map/ppermute | solution.py:458
  77.1 6.1 %collective-permute-start.23 = (bf16[32,3584]{1,0:T(8,128)(2,1)S(1)}, bf16[32,3584]{1,0:T(8,128)(2,1)S(1)}, u32[]{:S(2)}, u32[]{:S(2)}) collective-permute-start(bf16[32,3584]{1,0:T(8,128)(2,1)S(1)} %pad_maximum_fusion.5), channel_id=1, source_target_pairs={{0,1},{1,0},{2,3},{3,2},{4,5},{5,4},{6,7},{7,6},{8,9},{9,8},{10,11... | collective-permute-start | bytes 688136 | tf_op jit(solution)/shard_map/ppermute | solution.py:458
  79.1 6.1 %collective-permute-start.21 = (bf16[32,3584]{1,0:T(8,128)(2,1)S(1)}, bf16[32,3584]{1,0:T(8,128)(2,1)S(1)}, u32[]{:S(2)}, u32[]{:S(2)}) collective-permute-start(bf16[32,3584]{1,0:T(8,128)(2,1)S(1)} %pad_maximum_fusion.4), channel_id=1, source_target_pairs={{0,16},{8,24},{16,0},{24,8},{1,17},{9,25},{17,1},{25,9},{2,18},{10... | collective-permute-start | bytes 688136 | tf_op jit(solution)/shard_map/ppermute | solution.py:458
  83.3 2.0 %collective-permute-start.25 = (bf16[64,3584]{1,0:T(8,128)(2,1)S(1)}, bf16[64,3584]{1,0:T(8,128)(2,1)S(1)}, u32[]{:S(2)}, u32[]{:S(2)}) collective-permute-start(bf16[64,3584]{1,0:T(8,128)(2,1)S(1)} %pad_maximum_fusion.2.own_high), channel_id=1, source_target_pairs={{0,8},{8,0},{16,24},{24,16},{1,9},{9,1},{17,25},{25,17},{2,10},{10... | collective-permute-start | bytes 1376264 | tf_op jit(solution)/shard_map/ppermute | solution.py:458
  95.4 2.5 %collective-permute-start.26 = (bf16[64,7168]{1,0:T(8,128)(2,1)S(1)}, bf16[64,7168]{1,0:T(8,128)(2,1)S(1)}, u32[]{:S(2)}, u32[]{:S(2)}) collective-permute-start(bf16[64,7168]{1,0:T(8,128)(2,1)S(1)} %get-tuple-element.19), channel_id=1, source_target_pairs={{0,8},{8,0},{16,24},{24,16},{1,9},{9,1},{17,25},{25,17},{2,10},{10... | collective-permute-start | bytes 2752520 | tf_op jit(solution)/shard_map/ppermute | solution.py:458
  98.2 7.7 %collective-permute-start.29 = (bf16[32,3584]{1,0:T(8,128)(2,1)S(1)}, bf16[32,3584]{1,0:T(8,128)(2,1)S(1)}, u32[]{:S(2)}, u32[]{:S(2)}) collective-permute-start(bf16[32,3584]{1,0:T(8,128)(2,1)S(1)} %pad_maximum_fusion.6), channel_id=1, source_target_pairs={{0,1},{1,0},{2,3},{3,2},{4,5},{5,4},{6,7},{7,6},{8,9},{9,8},{10,11... | collective-permute-start | bytes 688136 | tf_op jit(solution)/shard_map/ppermute | solution.py:458
  99.7 7.7 %collective-permute-start.27 = (bf16[32,3584]{1,0:T(8,128)(2,1)S(1)}, bf16[32,3584]{1,0:T(8,128)(2,1)S(1)}, u32[]{:S(2)}, u32[]{:S(2)}) collective-permute-start(bf16[32,3584]{1,0:T(8,128)(2,1)S(1)} %slice.223), channel_id=1, source_target_pairs={{0,16},{8,24},{16,0},{24,8},{1,17},{9,25},{17,1},{25,9},{2,18},{10... | collective-permute-start | bytes 688136 | tf_op jit(solution)/shard_map/ppermute | solution.py:458
  106.0 4.9 %collective-permute-start.30 = (bf16[16,3584]{1,0:T(8,128)(2,1)S(1)}, bf16[16,3584]{1,0:T(8,128)(2,1)S(1)}, u32[]{:S(2)}, u32[]{:S(2)}) collective-permute-start(bf16[16,3584]{1,0:T(8,128)(2,1)S(1)} %slice.224), channel_id=1, source_target_pairs={{0,16},{8,24},{16,0},{24,8},{1,17},{9,25},{17,1},{25,9},{2,18},{10... | collective-permute-start | bytes 344072 | tf_op jit(solution)/shard_map/ppermute | solution.py:458
  107.4 4.9 %collective-permute-start.28 = (bf16[16,3584]{1,0:T(8,128)(2,1)S(1)}, bf16[16,3584]{1,0:T(8,128)(2,1)S(1)}, u32[]{:S(2)}, u32[]{:S(2)}) collective-permute-start(bf16[16,3584]{1,0:T(8,128)(2,1)S(1)} %slice.225), channel_id=1, source_target_pairs={{0,1},{1,0},{2,3},{3,2},{4,5},{5,4},{6,7},{7,6},{8,9},{9,8},{10,11... | collective-permute-start | bytes 344072 | tf_op jit(solution)/shard_map/ppermute | solution.py:458
  112.4 4.5 %collective-permute-start.31 = (bf16[4,7168]{1,0:T(4,128)(2,1)S(1)}, bf16[4,7168]{1,0:T(4,128)(2,1)S(1)}, u32[]{:S(2)}, u32[]{:S(2)}) collective-permute-start(bf16[4,7168]{1,0:T(4,128)(2,1)S(1)} %get-tuple-element.40), channel_id=1, source_target_pairs={{0,2},{1,3},{2,0},{3,1},{4,6},{5,7},{6,4},{7,5},{8,10},{9,11},{10,... | collective-permute-start | bytes 172040 | tf_op jit(solution)/shard_map/ppermute | solution.py:458
  112.5 5.8 %collective-permute-start.32 = (bf16[4,7168]{1,0:T(4,128)(2,1)S(1)}, bf16[4,7168]{1,0:T(4,128)(2,1)S(1)}, u32[]{:S(2)}, u32[]{:S(2)}) collective-permute-start(bf16[4,7168]{1,0:T(4,128)(2,1)S(1)} %get-tuple-element.42), channel_id=1, source_target_pairs={{0,4},{1,5},{2,6},{3,7},{4,0},{5,1},{6,2},{7,3},{8,12},{9,13},{10,... | collective-permute-start | bytes 172040 | tf_op jit(solution)/shard_map/ppermute | solution.py:458
  115.1 6.0 %collective-permute-start.33 = (bf16[4,7168]{1,0:T(4,128)(2,1)S(1)}, bf16[4,7168]{1,0:T(4,128)(2,1)S(1)}, u32[]{:S(2)}, u32[]{:S(2)}) collective-permute-start(bf16[4,7168]{1,0:T(4,128)(2,1)S(1)} %get-tuple-element.41), channel_id=1, source_target_pairs={{0,6},{1,7},{2,4},{3,5},{4,2},{5,3},{6,0},{7,1},{8,14},{9,15},{10,... | collective-permute-start | bytes 172040 | tf_op jit(solution)/shard_map/ppermute | solution.py:458
  (13 other events, 195.8 us)
where the time goes:
time: 122 us
  waiting for transfers between devices  56.7 us (46%)
  starting transfers between devices  35.1 us (29%)
  Pallas kernels  26.1 us (21%)
  other arithmetic  1.73 us (1%)
    ppermute x34, waiting for transfers between devices, move(): return lax.ppermute(value, axis, [(i, i ^ bit) for i in range(sizes[axis])])  56.7 us
    ppermute x34, starting transfers between devices, move(): return lax.ppermute(value, axis, [(i, i ^ bit) for i in range(sizes[axis])])  35.1 us
    pallas_call x1, Pallas kernels, attend(): pl.pallas_call(functools.partial(attend_kernel, chunk=chunk, scale=scale,...  12 us
    pallas_call x1, Pallas kernels, gated_mlp(): pl.pallas_call(functools.partial(mlp_kernel, chunk=chunk_of(middle, 1792)...  8.24 us
    pallas_call x1, Pallas kernels, out_proj(): pl.pallas_call(functools.partial(out_kernel, chunk=chunk_of(width, 3584),...  4.21 us
  transfers between devices with their start and end apart: 34, of which 22 were waited for; matrix products, arithmetic and copies ran while one was open for 1% of the time, Pallas kernels for 11%

commit v1 on v0

--- a/solution.py
+++ b/solution.py
@@ -356,9 +356,13 @@
 
 
 def gather_rows(rows, move, sizes):
+    def named(k, value, axis, bit):
+        return move(value, axis, bit * k)
+
     held = rows
     for axis, size, bit, ways in direct_phases(*sizes):
-        held = jnp.concatenate([held] + [move(held, axis, bit * k) for k in range(1, ways)], axis=0)
+        others = [named(k, held, axis, bit) for k in range(1, ways)]
+        held = jnp.concatenate([held] + others, axis=0)
     n, width = held.shape
     low, high = held[:, : width // 2], held[:, width // 2 :]
     low_x, high_y = move(low, "grp", 1), move(high, "rep", 2)
@@ -371,6 +375,10 @@
 
 
 def scatter_sum(low, high, send, move, sizes):
+    def named(k, value, axis, bit):
+        return move(value, axis, bit * k)
+
+
     def add(mine, theirs):
         return mine + theirs.astype(jnp.float32)
 
@@ -390,7 +398,8 @@
     for axis, size, bit, ways in reversed(direct_phases(*sizes)):
         per = total.shape[0] // ways
         moved = [
-            move(narrow(total[k * per : (k + 1) * per]), axis, bit * k) for k in range(1, ways)
+            named(k, narrow(total[k * per : (k + 1) * per]), axis, bit)
+            for k in range(1, ways)
         ]
         total = total[:per]
         for piece in moved:
@@ -399,6 +408,9 @@
 
 
 def to_heads(near, far, move, sizes):
+    def named(k, value, axis, bit):
+        return move(value, axis, bit * k)
+
     got = move(far, "grp", 1)
     order = [phase for phase in direct_phases(*sizes) if phase[0] == "grp"]
     high = near.shape[0]
@@ -409,23 +421,26 @@
         per = held.shape[0] // ways
         weight = per
         parts = [held[k * per : (k + 1) * per] for k in range(ways)]
-        parts = parts[:1] + [move(parts[k], axis, bit * k) for k in range(1, ways)]
-        named = [[sender + k * weight for sender in senders] for k in range(ways)]
+        parts = parts[:1] + [named(k, parts[k], axis, bit) for k in range(1, ways)]
+        places = [[sender + k * weight for sender in senders] for k in range(ways)]
         if n + 1 < len(order):
-            held, senders = jnp.concatenate(parts, axis=1), sum(named, [])
+            held, senders = jnp.concatenate(parts, axis=1), sum(places, [])
     return (
         [part.reshape(-1, part.shape[-1]) for part in parts],
-        tuple(tuple(names) for names in named),
+        tuple(tuple(names) for names in places),
     )
 
 
 def sum_heads(keep, send, move, sizes):
+    def named(k, value, axis, bit):
+        return move(value, axis, bit * k)
+
     got = move(send, "grp", 1)
     total = keep + got.astype(jnp.float32)
     for axis, size, bit, ways in [p for p in direct_phases(*sizes) if p[0] == "grp"]:
         per = total.shape[0] // ways
         moved = [
-            move(total[k * per : (k + 1) * per].astype(jnp.bfloat16), axis, bit * k)
+            named(k, total[k * per : (k + 1) * per].astype(jnp.bfloat16), axis, bit)
             for k in range(1, ways)
         ]
         total = total[:per]

time: 122 us -> 122 us (level)
  no operation moved by 1% of the time
where the time goes in v1:
time: 122 us
  waiting for transfers between devices  56.7 us (46%)
  starting transfers between devices  35.1 us (29%)
  Pallas kernels  26.1 us (21%)
  other arithmetic  1.73 us (1%)
    ppermute x34, waiting for transfers between devices, move(): return lax.ppermute(value, axis, [(i, i ^ bit) for i in range(sizes[axis])])  56.7 us
    ppermute x34, starting transfers between devices, move(): return lax.ppermute(value, axis, [(i, i ^ bit) for i in range(sizes[axis])])  35.1 us
    pallas_call x1, Pallas kernels, attend(): pl.pallas_call(functools.partial(attend_kernel, chunk=chunk, scale=scale,...  12 us
    pallas_call x1, Pallas kernels, gated_mlp(): pl.pallas_call(functools.partial(mlp_kernel, chunk=chunk_of(middle, 1792)...  8.24 us
    pallas_call x1, Pallas kernels, out_proj(): pl.pallas_call(functools.partial(out_kernel, chunk=chunk_of(width, 3584),...  4.21 us
  transfers between devices with their start and end apart: 34, of which 22 were waited for; matrix products, arithmetic and copies ran while one was open for 1% of the time, Pallas kernels for 11%

profile of v1, /device:TPU:0, one launch (start us, length us, event | category | flops | bytes accessed | tf_op | source)
XLA Modules:
  0.0 121.7 jit_solution(16331187033214274071)
XLA Ops:
  0.6 2.6 %collective-permute-start.4 = (bf16[4,8192]{1,0:T(4,128)(2,1)}, bf16[4,8192]{1,0:T(4,128)(2,1)S(1)}, u32[]{:S(2)}, u32[]{:S(2)}) collective-permute-start(bf16[4,8192]{1,0:T(4,128)(2,1)} %param.14), channel_id=1, source_target_pairs={{0,16},{8,24},{16,0},{24,8},{1,17},{9,25},{17,1},{25,9},{2,18},{10... | collective-permute-start | bytes 196616 | tf_op jit(solution)/shard_map/ppermute | solution.py:473
  3.2 1.7 %own_columns.1.refs_0_ = bf16[128,1024]{1,0:T(8,128)(2,1)} custom-call(s32[1]{0:T(128)} %bitcast.start.group, bf16[128,8192]{1,0:T(8,128)(2,1)} %source.1), custom_call_target="tpu_custom_call" | custom-call | bytes 524288 | tf_op jit(solution)/shard_map/own_columns/pallas_call | solution.py:192
  4.9 1.8 %collective-permute-start.1 = (bf16[128,1024]{1,0:T(8,128)(2,1)}, bf16[128,1024]{1,0:T(8,128)(2,1)S(1)}, u32[]{:S(2)}, u32[]{:S(2)}) collective-permute-start(bf16[128,1024]{1,0:T(8,128)(2,1)} %own_columns.1.refs_0_), channel_id=1, source_target_pairs={{0,16},{8,24},{16,0},{24,8},{1,17},{9,25},{17,1},{25,9},{2,18},{10... | collective-permute-start | bytes 786440 | tf_op jit(solution)/shard_map/ppermute | solution.py:473
  9.0 1.4 %collective-permute-start.7 = (bf16[4,64,128]{2,1,0:T(8,128)(2,1)S(1)}, bf16[4,64,128]{2,1,0:T(8,128)(2,1)S(1)}, u32[]{:S(2)}, u32[]{:S(2)}) collective-permute-start(bf16[4,64,128]{2,1,0:T(8,128)(2,1)S(1)} %get-tuple-element.37), channel_id=1, source_target_pairs={{0,16},{8,24},{16,0},{24,8},{1,17},{9,25},{17,1},{25,9},{2,18},{10... | collective-permute-start | bytes 196616 | tf_op jit(solution)/shard_map/ppermute | solution.py:473
  10.7 5.0 %collective-permute-done.7.refs_2_ = bf16[4,64,128]{2,1,0:T(8,128)(2,1)S(1)} collective-permute-done((bf16[4,64,128]{2,1,0:T(8,128)(2,1)S(1)}, bf16[4,64,128]{2,1,0:T(8,128)(2,1)S(1)}, u32[]{:S(2)}, u32[]{:S(2)}) %collective-permute-start.7) | collective-permute-done | bytes 65568 | tf_op jit(solution)/shard_map/ppermute | solution.py:473
  15.9 12.0 %attend.1 = (bf16[4,32,512]{2,1,0:T(8,128)(2,1)S(1)}, bf16[4,32,512]{2,1,0:T(8,128)(2,1)S(1)}, bf16[1024,7168]{1,0:T(8,128)(2,1)S(1)}) custom-call(s32[4]{0:T(128)S(1)} %copy-done.3, s32[4]{0:T(128)S(1)} %iota_xor_fusion.place, s32[1]{0:T(128)} %bitcast.start.group, bf16[4,64,128]{2,1,0:T(8,128)(2,1)S(1)} %get-tuple-element.39.refs_0_, ...), custom_call_target="tpu_custom_call" | custom-call | flops 2415919104 | bytes 18874368 | tf_op jit(solution)/shard_map/attend/pallas_call | solution.py:154
  28.6 4.4 %collective-permute-done.9 = bf16[4,32,512]{2,1,0:T(8,128)(2,1)S(1)} collective-permute-done((bf16[4,32,512]{2,1,0:T(8,128)(2,1)S(1)}, bf16[4,32,512]{2,1,0:T(8,128)(2,1)S(1)}, u32[]{:S(2)}, u32[]{:S(2)}) %collective-permute-start.9) | collective-permute-done | bytes 131104 | tf_op jit(solution)/shard_map/ppermute | solution.py:473
  35.4 2.0 %collective-permute-start.12 = (bf16[1,2,32,512]{3,2,0,1:T(8,128)(2,1)S(1)}, bf16[1,2,32,512]{3,2,0,1:T(8,128)(2,1)S(1)}, u32[]{:S(2)}, u32[]{:S(2)}) collective-permute-start(bf16[1,2,32,512]{3,2,0,1:T(8,128)(2,1)S(1)} %get-tuple-element.32), channel_id=1, source_target_pairs={{0,6},{1,7},{2,4},{3,5},{4,2},{5,3},{6,0},{7,1},{8,14},{9,15},{10,... | collective-permute-start | bytes 196616 | tf_op jit(solution)/shard_map/ppermute | solution.py:473
  38.0 4.2 %collective-permute-done.11 = bf16[1,2,32,512]{3,2,0,1:T(8,128)(2,1)S(1)} collective-permute-done((bf16[1,2,32,512]{3,2,0,1:T(8,128)(2,1)S(1)}, bf16[1,2,32,512]{3,2,0,1:T(8,128)(2,1)S(1)}, u32[]{:S(2)}, u32[]{:S(2)}) %collective-permute-start.11) | collective-permute-done | bytes 65568 | tf_op jit(solution)/shard_map/ppermute | solution.py:473
  42.3 4.2 %out_proj.1 = (f32[16,7168]{1,0:T(8,128)S(1)}, bf16[16,7168]{1,0:T(8,128)(2,1)S(1)}) custom-call(s32[4]{0:T(128)S(1)} %iota_xor_fusion.place, bf16[128,1024]{1,0:T(8,128)(2,1)S(1)} %copy-done.2, bf16[128,1024]{1,0:T(8,128)(2,1)S(1)} %collective-permute-done.refs_1_, bf16[128,1024]{1,0:T(8,128)(2,1)S(1)} %collective-permute-done.1.refs_2_, ...), custom_call_target="tpu_custom_call" | custom-call | flops 469762048 | bytes 14680064 | tf_op jit(solution)/shard_map/out_proj/pallas_call | solution.py:237
  46.8 6.6 %collective-permute-done.13 = bf16[16,7168]{1,0:T(8,128)(2,1)S(1)} collective-permute-done((bf16[16,7168]{1,0:T(8,128)(2,1)S(1)}, bf16[16,7168]{1,0:T(8,128)(2,1)S(1)}, u32[]{:S(2)}, u32[]{:S(2)}) %collective-permute-start.13) | collective-permute-done | bytes 229408 | tf_op jit(solution)/shard_map/ppermute | solution.py:473
  53.6 2.4 %collective-permute-start.14 = (bf16[4,7168]{1,0:T(4,128)(2,1)S(1)}, bf16[4,7168]{1,0:T(4,128)(2,1)S(1)}, u32[]{:S(2)}, u32[]{:S(2)}) collective-permute-start(bf16[4,7168]{1,0:T(4,128)(2,1)S(1)} %get-tuple-element.47), channel_id=1, source_target_pairs={{0,2},{1,3},{2,0},{3,1},{4,6},{5,7},{6,4},{7,5},{8,10},{9,11},{10,... | collective-permute-start | bytes 172040 | tf_op jit(solution)/shard_map/ppermute | solution.py:473
  57.0 1.4 %collective-permute-start.16 = (bf16[4,7168]{1,0:T(4,128)(2,1)S(1)}, bf16[4,7168]{1,0:T(4,128)(2,1)S(1)}, u32[]{:S(2)}, u32[]{:S(2)}) collective-permute-start(bf16[4,7168]{1,0:T(4,128)(2,1)S(1)} %get-tuple-element.48), channel_id=1, source_target_pairs={{0,6},{1,7},{2,4},{3,5},{4,2},{5,3},{6,0},{7,1},{8,14},{9,15},{10,... | collective-permute-start | bytes 172040 | tf_op jit(solution)/shard_map/ppermute | solution.py:473
  58.4 3.7 %collective-permute-done.15 = bf16[4,7168]{1,0:T(4,128)(2,1)S(1)} collective-permute-done((bf16[4,7168]{1,0:T(4,128)(2,1)S(1)}, bf16[4,7168]{1,0:T(4,128)(2,1)S(1)}, u32[]{:S(2)}, u32[]{:S(2)}) %collective-permute-start.15) | collective-permute-done | bytes 57376 | tf_op jit(solution)/shard_map/ppermute | solution.py:473
  64.3 1.8 %collective-permute-start.18 = (bf16[4,7168]{1,0:T(4,128)(2,1)S(1)}, bf16[4,7168]{1,0:T(4,128)(2,1)S(1)}, u32[]{:S(2)}, u32[]{:S(2)}) collective-permute-start(bf16[4,7168]{1,0:T(4,128)(2,1)S(1)} %fusion.9), channel_id=1, source_target_pairs={{0,4},{1,5},{2,6},{3,7},{4,0},{5,1},{6,2},{7,3},{8,12},{9,13},{10,... | collective-permute-start | bytes 172040 | tf_op jit(solution)/shard_map/ppermute | solution.py:473
  66.1 1.8 %collective-permute-start.19 = (bf16[4,7168]{1,0:T(4,128)(2,1)S(1)}, bf16[4,7168]{1,0:T(4,128)(2,1)S(1)}, u32[]{:S(2)}, u32[]{:S(2)}) collective-permute-start(bf16[4,7168]{1,0:T(4,128)(2,1)S(1)} %fusion.9), channel_id=1, source_target_pairs={{0,6},{1,7},{2,4},{3,5},{4,2},{5,3},{6,0},{7,1},{8,14},{9,15},{10,... | collective-permute-start | bytes 172040 | tf_op jit(solution)/shard_map/ppermute | solution.py:473
  67.9 2.5 %collective-permute-done.18 = bf16[4,7168]{1,0:T(4,128)(2,1)S(1)} collective-permute-done((bf16[4,7168]{1,0:T(4,128)(2,1)S(1)}, bf16[4,7168]{1,0:T(4,128)(2,1)S(1)}, u32[]{:S(2)}, u32[]{:S(2)}) %collective-permute-start.18) | collective-permute-done | bytes 57376 | tf_op jit(solution)/shard_map/ppermute | solution.py:473
  70.4 1.7 %collective-permute-done.19 = bf16[4,7168]{1,0:T(4,128)(2,1)S(1)} collective-permute-done((bf16[4,7168]{1,0:T(4,128)(2,1)S(1)}, bf16[4,7168]{1,0:T(4,128)(2,1)S(1)}, u32[]{:S(2)}, u32[]{:S(2)}) %collective-permute-start.19) | collective-permute-done | bytes 57376 | tf_op jit(solution)/shard_map/ppermute | solution.py:473
  74.4 2.7 %collective-permute-done.22 = bf16[16,3584]{1,0:T(8,128)(2,1)S(1)} collective-permute-done((bf16[16,3584]{1,0:T(8,128)(2,1)S(1)}, bf16[16,3584]{1,0:T(8,128)(2,1)S(1)}, u32[]{:S(2)}, u32[]{:S(2)}) %collective-permute-start.22) | collective-permute-done | bytes 114720 | tf_op jit(solution)/shard_map/ppermute | solution.py:473
  80.5 2.8 %collective-permute-done.23 = bf16[32,3584]{1,0:T(8,128)(2,1)S(1)} collective-permute-done((bf16[32,3584]{1,0:T(8,128)(2,1)S(1)}, bf16[32,3584]{1,0:T(8,128)(2,1)S(1)}, u32[]{:S(2)}, u32[]{:S(2)}) %collective-permute-start.23) | collective-permute-done | bytes 229408 | tf_op jit(solution)/shard_map/ppermute | solution.py:473
  83.4 1.8 %collective-permute-done.21 = bf16[32,3584]{1,0:T(8,128)(2,1)S(1)} collective-permute-done((bf16[32,3584]{1,0:T(8,128)(2,1)S(1)}, bf16[32,3584]{1,0:T(8,128)(2,1)S(1)}, u32[]{:S(2)}, u32[]{:S(2)}) %collective-permute-start.21) | collective-permute-done | bytes 229408 | tf_op jit(solution)/shard_map/ppermute | solution.py:473
  85.3 1.8 %collective-permute-done.24.other_low = bf16[64,3584]{1,0:T(8,128)(2,1)S(1)} collective-permute-done((bf16[64,3584]{1,0:T(8,128)(2,1)S(1)}, bf16[64,3584]{1,0:T(8,128)(2,1)S(1)}, u32[]{:S(2)}, u32[]{:S(2)}) %collective-permute-start.24) | collective-permute-done | bytes 458784 | tf_op jit(solution)/shard_map/ppermute | solution.py:473
  87.1 8.2 %gated_mlp.1 = (f32[64,3584]{1,0:T(8,128)S(1)}, f32[64,3584]{1,0:T(8,128)S(1)}, bf16[64,7168]{1,0:T(8,128)(2,1)S(1)}) custom-call(bf16[64,3584]{1,0:T(8,128)(2,1)S(1)} %pad_maximum_fusion.1.own_low, bf16[64,3584]{1,0:T(8,128)(2,1)S(1)} %pad_maximum_fusion.2.own_high, bf16[64,3584]{1,0:T(8,128)(2,1)S(1)} %collective-permute-done.24.other_low, ...), custom_call_target="tpu_custom_call" | custom-call | flops 3170893824 | bytes 24772608 | tf_op jit(solution)/shard_map/gated_mlp/pallas_call | solution.py:320
  95.6 2.4 %collective-permute-done.26 = bf16[64,7168]{1,0:T(8,128)(2,1)S(1)} collective-permute-done((bf16[64,7168]{1,0:T(8,128)(2,1)S(1)}, bf16[64,7168]{1,0:T(8,128)(2,1)S(1)}, u32[]{:S(2)}, u32[]{:S(2)}) %collective-permute-start.26) | collective-permute-done | bytes 917536 | tf_op jit(solution)/shard_map/ppermute | solution.py:473
  98.2 1.4 %collective-permute-start.29 = (bf16[32,3584]{1,0:T(8,128)(2,1)S(1)}, bf16[32,3584]{1,0:T(8,128)(2,1)S(1)}, u32[]{:S(2)}, u32[]{:S(2)}) collective-permute-start(bf16[32,3584]{1,0:T(8,128)(2,1)S(1)} %pad_maximum_fusion.6), channel_id=1, source_target_pairs={{0,1},{1,0},{2,3},{3,2},{4,5},{5,4},{6,7},{7,6},{8,9},{9,8},{10,11... | collective-permute-start | bytes 688136 | tf_op jit(solution)/shard_map/ppermute | solution.py:473
  100.4 5.5 %collective-permute-done.29 = bf16[32,3584]{1,0:T(8,128)(2,1)S(1)} collective-permute-done((bf16[32,3584]{1,0:T(8,128)(2,1)S(1)}, bf16[32,3584]{1,0:T(8,128)(2,1)S(1)}, u32[]{:S(2)}, u32[]{:S(2)}) %collective-permute-start.29) | collective-permute-done | bytes 229408 | tf_op jit(solution)/shard_map/ppermute | solution.py:473
  108.2 2.6 %collective-permute-done.30 = bf16[16,3584]{1,0:T(8,128)(2,1)S(1)} collective-permute-done((bf16[16,3584]{1,0:T(8,128)(2,1)S(1)}, bf16[16,3584]{1,0:T(8,128)(2,1)S(1)}, u32[]{:S(2)}, u32[]{:S(2)}) %collective-permute-start.30) | collective-permute-done | bytes 114720 | tf_op jit(solution)/shard_map/ppermute | solution.py:473
  110.8 1.4 %collective-permute-done.28 = bf16[16,3584]{1,0:T(8,128)(2,1)S(1)} collective-permute-done((bf16[16,3584]{1,0:T(8,128)(2,1)S(1)}, bf16[16,3584]{1,0:T(8,128)(2,1)S(1)}, u32[]{:S(2)}, u32[]{:S(2)}) %collective-permute-start.28) | collective-permute-done | bytes 114720 | tf_op jit(solution)/shard_map/ppermute | solution.py:473
  112.5 2.6 %collective-permute-start.32 = (bf16[4,7168]{1,0:T(4,128)(2,1)S(1)}, bf16[4,7168]{1,0:T(4,128)(2,1)S(1)}, u32[]{:S(2)}, u32[]{:S(2)}) collective-permute-start(bf16[4,7168]{1,0:T(4,128)(2,1)S(1)} %get-tuple-element.42), channel_id=1, source_target_pairs={{0,4},{1,5},{2,6},{3,7},{4,0},{5,1},{6,2},{7,3},{8,12},{9,13},{10,... | collective-permute-start | bytes 172040 | tf_op jit(solution)/shard_map/ppermute | solution.py:473
  115.1 1.8 %collective-permute-start.33 = (bf16[4,7168]{1,0:T(4,128)(2,1)S(1)}, bf16[4,7168]{1,0:T(4,128)(2,1)S(1)}, u32[]{:S(2)}, u32[]{:S(2)}) collective-permute-start(bf16[4,7168]{1,0:T(4,128)(2,1)S(1)} %get-tuple-element.41), channel_id=1, source_target_pairs={{0,6},{1,7},{2,4},{3,5},{4,2},{5,3},{6,0},{7,1},{8,14},{9,15},{10,... | collective-permute-start | bytes 172040 | tf_op jit(solution)/shard_map/ppermute | solution.py:473
  116.8 1.4 %collective-permute-done.32 = bf16[4,7168]{1,0:T(4,128)(2,1)S(1)} collective-permute-done((bf16[4,7168]{1,0:T(4,128)(2,1)S(1)}, bf16[4,7168]{1,0:T(4,128)(2,1)S(1)}, u32[]{:S(2)}, u32[]{:S(2)}) %collective-permute-start.32) | collective-permute-done | bytes 57376 | tf_op jit(solution)/shard_map/ppermute | solution.py:473
  118.2 2.8 %collective-permute-done.33 = bf16[4,7168]{1,0:T(4,128)(2,1)S(1)} collective-permute-done((bf16[4,7168]{1,0:T(4,128)(2,1)S(1)}, bf16[4,7168]{1,0:T(4,128)(2,1)S(1)}, u32[]{:S(2)}, u32[]{:S(2)}) %collective-permute-start.33) | collective-permute-done | bytes 57376 | tf_op jit(solution)/shard_map/ppermute | solution.py:473
  (97 shorter events, 21.0 us)
Async XLA Ops:
  0.0 6.8 %collective-permute-start.3 = (bf16[4,8192]{1,0:T(4,128)(2,1)}, bf16[4,8192]{1,0:T(4,128)(2,1)S(1)}, u32[]{:S(2)}, u32[]{:S(2)}) collective-permute-start(bf16[4,8192]{1,0:T(4,128)(2,1)} %param.14), channel_id=1, source_target_pairs={{0,8},{8,0},{16,24},{24,16},{1,9},{9,1},{17,25},{25,17},{2,10},{10... | collective-permute-start | bytes 196616 | tf_op jit(solution)/shard_map/ppermute | solution.py:473
  0.6 6.3 %collective-permute-start.4 = (bf16[4,8192]{1,0:T(4,128)(2,1)}, bf16[4,8192]{1,0:T(4,128)(2,1)S(1)}, u32[]{:S(2)}, u32[]{:S(2)}) collective-permute-start(bf16[4,8192]{1,0:T(4,128)(2,1)} %param.14), channel_id=1, source_target_pairs={{0,16},{8,24},{16,0},{24,8},{1,17},{9,25},{17,1},{25,9},{2,18},{10... | collective-permute-start | bytes 196616 | tf_op jit(solution)/shard_map/ppermute | solution.py:473
  3.2 4.3 %collective-permute-start.5 = (bf16[4,8192]{1,0:T(4,128)(2,1)}, bf16[4,8192]{1,0:T(4,128)(2,1)S(1)}, u32[]{:S(2)}, u32[]{:S(2)}) collective-permute-start(bf16[4,8192]{1,0:T(4,128)(2,1)} %param.14), channel_id=1, source_target_pairs={{0,24},{8,16},{16,8},{24,0},{1,25},{9,17},{17,9},{25,1},{2,26},{10... | collective-permute-start | bytes 196616 | tf_op jit(solution)/shard_map/ppermute | solution.py:473
  4.9 23.2 %collective-permute-start.1 = (bf16[128,1024]{1,0:T(8,128)(2,1)}, bf16[128,1024]{1,0:T(8,128)(2,1)S(1)}, u32[]{:S(2)}, u32[]{:S(2)}) collective-permute-start(bf16[128,1024]{1,0:T(8,128)(2,1)} %own_columns.1.refs_0_), channel_id=1, source_target_pairs={{0,16},{8,24},{16,0},{24,8},{1,17},{9,25},{17,1},{25,9},{2,18},{10... | collective-permute-start | bytes 786440 | tf_op jit(solution)/shard_map/ppermute | solution.py:473
  9.0 6.7 %collective-permute-start.7 = (bf16[4,64,128]{2,1,0:T(8,128)(2,1)S(1)}, bf16[4,64,128]{2,1,0:T(8,128)(2,1)S(1)}, u32[]{:S(2)}, u32[]{:S(2)}) collective-permute-start(bf16[4,64,128]{2,1,0:T(8,128)(2,1)S(1)} %get-tuple-element.37), channel_id=1, source_target_pairs={{0,16},{8,24},{16,0},{24,8},{1,17},{9,25},{17,1},{25,9},{2,18},{10... | collective-permute-start | bytes 196616 | tf_op jit(solution)/shard_map/ppermute | solution.py:473
  10.4 5.5 %collective-permute-start.8 = (bf16[4,64,128]{2,1,0:T(8,128)(2,1)S(1)}, bf16[4,64,128]{2,1,0:T(8,128)(2,1)S(1)}, u32[]{:S(2)}, u32[]{:S(2)}) collective-permute-start(bf16[4,64,128]{2,1,0:T(8,128)(2,1)S(1)} %get-tuple-element.36), channel_id=1, source_target_pairs={{0,24},{8,16},{16,8},{24,0},{1,25},{9,17},{17,9},{25,1},{2,26},{10... | collective-permute-start | bytes 196616 | tf_op jit(solution)/shard_map/ppermute | solution.py:473
  27.9 5.0 %collective-permute-start.9 = (bf16[4,32,512]{2,1,0:T(8,128)(2,1)S(1)}, bf16[4,32,512]{2,1,0:T(8,128)(2,1)S(1)}, u32[]{:S(2)}, u32[]{:S(2)}) collective-permute-start(bf16[4,32,512]{2,1,0:T(8,128)(2,1)S(1)} %get-tuple-element.14), channel_id=1, source_target_pairs={{0,1},{1,0},{2,3},{3,2},{4,5},{5,4},{6,7},{7,6},{8,9},{9,8},{10,11... | collective-permute-start | bytes 393224 | tf_op jit(solution)/shard_map/ppermute | solution.py:473
  28.0 9.4 %collective-permute-start = (bf16[128,1024]{1,0:T(8,128)(2,1)S(1)}, bf16[128,1024]{1,0:T(8,128)(2,1)S(1)}, u32[]{:S(2)}, u32[]{:S(2)}) collective-permute-start(bf16[128,1024]{1,0:T(8,128)(2,1)S(1)} %copy-done.2), channel_id=1, source_target_pairs={{0,8},{8,0},{16,24},{24,16},{1,9},{9,1},{17,25},{25,17},{2,10},{10... | collective-permute-start | bytes 786440 | tf_op jit(solution)/shard_map/ppermute | solution.py:473
  28.1 14.2 %collective-permute-start.2 = (bf16[128,1024]{1,0:T(8,128)(2,1)S(1)}, bf16[128,1024]{1,0:T(8,128)(2,1)S(1)}, u32[]{:S(2)}, u32[]{:S(2)}) collective-permute-start(bf16[128,1024]{1,0:T(8,128)(2,1)S(1)} %collective-permute-done.1.refs_2_), channel_id=1, source_target_pairs={{0,8},{8,0},{16,24},{24,16},{1,9},{9,1},{17,25},{25,17},{2,10},{10... | collective-permute-start | bytes 786440 | tf_op jit(solution)/shard_map/ppermute | solution.py:473
  33.0 5.0 %collective-permute-start.10 = (bf16[1,2,32,512]{3,2,0,1:T(8,128)(2,1)S(1)}, bf16[1,2,32,512]{3,2,0,1:T(8,128)(2,1)S(1)}, u32[]{:S(2)}, u32[]{:S(2)}) collective-permute-start(bf16[1,2,32,512]{3,2,0,1:T(8,128)(2,1)S(1)} %get-tuple-element.34), channel_id=1, source_target_pairs={{0,2},{1,3},{2,0},{3,1},{4,6},{5,7},{6,4},{7,5},{8,10},{9,11},{10,... | collective-permute-start | bytes 196616 | tf_op jit(solution)/shard_map/ppermute | solution.py:473
  34.1 8.1 %collective-permute-start.11 = (bf16[1,2,32,512]{3,2,0,1:T(8,128)(2,1)S(1)}, bf16[1,2,32,512]{3,2,0,1:T(8,128)(2,1)S(1)}, u32[]{:S(2)}, u32[]{:S(2)}) collective-permute-start(bf16[1,2,32,512]{3,2,0,1:T(8,128)(2,1)S(1)} %get-tuple-element.35), channel_id=1, source_target_pairs={{0,4},{1,5},{2,6},{3,7},{4,0},{5,1},{6,2},{7,3},{8,12},{9,13},{10,... | collective-permute-start | bytes 196616 | tf_op jit(solution)/shard_map/ppermute | solution.py:473
  35.4 6.8 %collective-permute-start.12 = (bf16[1,2,32,512]{3,2,0,1:T(8,128)(2,1)S(1)}, bf16[1,2,32,512]{3,2,0,1:T(8,128)(2,1)S(1)}, u32[]{:S(2)}, u32[]{:S(2)}) collective-permute-start(bf16[1,2,32,512]{3,2,0,1:T(8,128)(2,1)S(1)} %get-tuple-element.32), channel_id=1, source_target_pairs={{0,6},{1,7},{2,4},{3,5},{4,2},{5,3},{6,0},{7,1},{8,14},{9,15},{10,... | collective-permute-start | bytes 196616 | tf_op jit(solution)/shard_map/ppermute | solution.py:473
  46.5 6.9 %collective-permute-start.13 = (bf16[16,7168]{1,0:T(8,128)(2,1)S(1)}, bf16[16,7168]{1,0:T(8,128)(2,1)S(1)}, u32[]{:S(2)}, u32[]{:S(2)}) collective-permute-start(bf16[16,7168]{1,0:T(8,128)(2,1)S(1)} %get-tuple-element.17), channel_id=1, source_target_pairs={{0,1},{1,0},{2,3},{3,2},{4,5},{5,4},{6,7},{7,6},{8,9},{9,8},{10,11... | collective-permute-start | bytes 688136 | tf_op jit(solution)/shard_map/ppermute | solution.py:473
  53.6 4.8 %collective-permute-start.14 = (bf16[4,7168]{1,0:T(4,128)(2,1)S(1)}, bf16[4,7168]{1,0:T(4,128)(2,1)S(1)}, u32[]{:S(2)}, u32[]{:S(2)}) collective-permute-start(bf16[4,7168]{1,0:T(4,128)(2,1)S(1)} %get-tuple-element.47), channel_id=1, source_target_pairs={{0,2},{1,3},{2,0},{3,1},{4,6},{5,7},{6,4},{7,5},{8,10},{9,11},{10,... | collective-permute-start | bytes 172040 | tf_op jit(solution)/shard_map/ppermute | solution.py:473
  56.0 6.2 %collective-permute-start.15 = (bf16[4,7168]{1,0:T(4,128)(2,1)S(1)}, bf16[4,7168]{1,0:T(4,128)(2,1)S(1)}, u32[]{:S(2)}, u32[]{:S(2)}) collective-permute-start(bf16[4,7168]{1,0:T(4,128)(2,1)S(1)} %get-tuple-element.49), channel_id=1, source_target_pairs={{0,4},{1,5},{2,6},{3,7},{4,0},{5,1},{6,2},{7,3},{8,12},{9,13},{10,... | collective-permute-start | bytes 172040 | tf_op jit(solution)/shard_map/ppermute | solution.py:473
  57.0 6.1 %collective-permute-start.16 = (bf16[4,7168]{1,0:T(4,128)(2,1)S(1)}, bf16[4,7168]{1,0:T(4,128)(2,1)S(1)}, u32[]{:S(2)}, u32[]{:S(2)}) collective-permute-start(bf16[4,7168]{1,0:T(4,128)(2,1)S(1)} %get-tuple-element.48), channel_id=1, source_target_pairs={{0,6},{1,7},{2,4},{3,5},{4,2},{5,3},{6,0},{7,1},{8,14},{9,15},{10,... | collective-permute-start | bytes 172040 | tf_op jit(solution)/shard_map/ppermute | solution.py:473
  63.4 4.5 %collective-permute-start.17 = (bf16[4,7168]{1,0:T(4,128)(2,1)S(1)}, bf16[4,7168]{1,0:T(4,128)(2,1)S(1)}, u32[]{:S(2)}, u32[]{:S(2)}) collective-permute-start(bf16[4,7168]{1,0:T(4,128)(2,1)S(1)} %fusion.9), channel_id=1, source_target_pairs={{0,2},{1,3},{2,0},{3,1},{4,6},{5,7},{6,4},{7,5},{8,10},{9,11},{10,... | collective-permute-start | bytes 172040 | tf_op jit(solution)/shard_map/ppermute | solution.py:473
  64.3 6.1 %collective-permute-start.18 = (bf16[4,7168]{1,0:T(4,128)(2,1)S(1)}, bf16[4,7168]{1,0:T(4,128)(2,1)S(1)}, u32[]{:S(2)}, u32[]{:S(2)}) collective-permute-start(bf16[4,7168]{1,0:T(4,128)(2,1)S(1)} %fusion.9), channel_id=1, source_target_pairs={{0,4},{1,5},{2,6},{3,7},{4,0},{5,1},{6,2},{7,3},{8,12},{9,13},{10,... | collective-permute-start | bytes 172040 | tf_op jit(solution)/shard_map/ppermute | solution.py:473
  66.1 6.0 %collective-permute-start.19 = (bf16[4,7168]{1,0:T(4,128)(2,1)S(1)}, bf16[4,7168]{1,0:T(4,128)(2,1)S(1)}, u32[]{:S(2)}, u32[]{:S(2)}) collective-permute-start(bf16[4,7168]{1,0:T(4,128)(2,1)S(1)} %fusion.9), channel_id=1, source_target_pairs={{0,6},{1,7},{2,4},{3,5},{4,2},{5,3},{6,0},{7,1},{8,14},{9,15},{10,... | collective-permute-start | bytes 172040 | tf_op jit(solution)/shard_map/ppermute | solution.py:473
  72.3 4.9 %collective-permute-start.22 = (bf16[16,3584]{1,0:T(8,128)(2,1)S(1)}, bf16[16,3584]{1,0:T(8,128)(2,1)S(1)}, u32[]{:S(2)}, u32[]{:S(2)}) collective-permute-start(bf16[16,3584]{1,0:T(8,128)(2,1)S(1)} %get-tuple-element.45), channel_id=1, source_target_pairs={{0,16},{8,24},{16,0},{24,8},{1,17},{9,25},{17,1},{25,9},{2,18},{10... | collective-permute-start | bytes 344072 | tf_op jit(solution)/shard_map/ppermute | solution.py:473
  73.1 6.0 %collective-permute-start.20 = (bf16[16,3584]{1,0:T(8,128)(2,1)S(1)}, bf16[16,3584]{1,0:T(8,128)(2,1)S(1)}, u32[]{:S(2)}, u32[]{:S(2)}) collective-permute-start(bf16[16,3584]{1,0:T(8,128)(2,1)S(1)} %get-tuple-element.46), channel_id=1, source_target_pairs={{0,1},{1,0},{2,3},{3,2},{4,5},{5,4},{6,7},{7,6},{8,9},{9,8},{10,11... | collective-permute-start | bytes 344072 | tf_op jit(solution)/shard_map/ppermute | solution.py:473
  77.1 6.1 %collective-permute-start.23 = (bf16[32,3584]{1,0:T(8,128)(2,1)S(1)}, bf16[32,3584]{1,0:T(8,128)(2,1)S(1)}, u32[]{:S(2)}, u32[]{:S(2)}) collective-permute-start(bf16[32,3584]{1,0:T(8,128)(2,1)S(1)} %pad_maximum_fusion.5), channel_id=1, source_target_pairs={{0,1},{1,0},{2,3},{3,2},{4,5},{5,4},{6,7},{7,6},{8,9},{9,8},{10,11... | collective-permute-start | bytes 688136 | tf_op jit(solution)/shard_map/ppermute | solution.py:473
  79.1 6.1 %collective-permute-start.21 = (bf16[32,3584]{1,0:T(8,128)(2,1)S(1)}, bf16[32,3584]{1,0:T(8,128)(2,1)S(1)}, u32[]{:S(2)}, u32[]{:S(2)}) collective-permute-start(bf16[32,3584]{1,0:T(8,128)(2,1)S(1)} %pad_maximum_fusion.4), channel_id=1, source_target_pairs={{0,16},{8,24},{16,0},{24,8},{1,17},{9,25},{17,1},{25,9},{2,18},{10... | collective-permute-start | bytes 688136 | tf_op jit(solution)/shard_map/ppermute | solution.py:473
  83.3 2.0 %collective-permute-start.25 = (bf16[64,3584]{1,0:T(8,128)(2,1)S(1)}, bf16[64,3584]{1,0:T(8,128)(2,1)S(1)}, u32[]{:S(2)}, u32[]{:S(2)}) collective-permute-start(bf16[64,3584]{1,0:T(8,128)(2,1)S(1)} %pad_maximum_fusion.2.own_high), channel_id=1, source_target_pairs={{0,8},{8,0},{16,24},{24,16},{1,9},{9,1},{17,25},{25,17},{2,10},{10... | collective-permute-start | bytes 1376264 | tf_op jit(solution)/shard_map/ppermute | solution.py:473
  95.4 2.5 %collective-permute-start.26 = (bf16[64,7168]{1,0:T(8,128)(2,1)S(1)}, bf16[64,7168]{1,0:T(8,128)(2,1)S(1)}, u32[]{:S(2)}, u32[]{:S(2)}) collective-permute-start(bf16[64,7168]{1,0:T(8,128)(2,1)S(1)} %get-tuple-element.19), channel_id=1, source_target_pairs={{0,8},{8,0},{16,24},{24,16},{1,9},{9,1},{17,25},{25,17},{2,10},{10... | collective-permute-start | bytes 2752520 | tf_op jit(solution)/shard_map/ppermute | solution.py:473
  98.2 7.7 %collective-permute-start.29 = (bf16[32,3584]{1,0:T(8,128)(2,1)S(1)}, bf16[32,3584]{1,0:T(8,128)(2,1)S(1)}, u32[]{:S(2)}, u32[]{:S(2)}) collective-permute-start(bf16[32,3584]{1,0:T(8,128)(2,1)S(1)} %pad_maximum_fusion.6), channel_id=1, source_target_pairs={{0,1},{1,0},{2,3},{3,2},{4,5},{5,4},{6,7},{7,6},{8,9},{9,8},{10,11... | collective-permute-start | bytes 688136 | tf_op jit(solution)/shard_map/ppermute | solution.py:473
  99.7 7.7 %collective-permute-start.27 = (bf16[32,3584]{1,0:T(8,128)(2,1)S(1)}, bf16[32,3584]{1,0:T(8,128)(2,1)S(1)}, u32[]{:S(2)}, u32[]{:S(2)}) collective-permute-start(bf16[32,3584]{1,0:T(8,128)(2,1)S(1)} %slice.223), channel_id=1, source_target_pairs={{0,16},{8,24},{16,0},{24,8},{1,17},{9,25},{17,1},{25,9},{2,18},{10... | collective-permute-start | bytes 688136 | tf_op jit(solution)/shard_map/ppermute | solution.py:473
  106.0 4.9 %collective-permute-start.30 = (bf16[16,3584]{1,0:T(8,128)(2,1)S(1)}, bf16[16,3584]{1,0:T(8,128)(2,1)S(1)}, u32[]{:S(2)}, u32[]{:S(2)}) collective-permute-start(bf16[16,3584]{1,0:T(8,128)(2,1)S(1)} %slice.224), channel_id=1, source_target_pairs={{0,16},{8,24},{16,0},{24,8},{1,17},{9,25},{17,1},{25,9},{2,18},{10... | collective-permute-start | bytes 344072 | tf_op jit(solution)/shard_map/ppermute | solution.py:473
  107.4 4.9 %collective-permute-start.28 = (bf16[16,3584]{1,0:T(8,128)(2,1)S(1)}, bf16[16,3584]{1,0:T(8,128)(2,1)S(1)}, u32[]{:S(2)}, u32[]{:S(2)}) collective-permute-start(bf16[16,3584]{1,0:T(8,128)(2,1)S(1)} %slice.225), channel_id=1, source_target_pairs={{0,1},{1,0},{2,3},{3,2},{4,5},{5,4},{6,7},{7,6},{8,9},{9,8},{10,11... | collective-permute-start | bytes 344072 | tf_op jit(solution)/shard_map/ppermute | solution.py:473
  112.4 4.5 %collective-permute-start.31 = (bf16[4,7168]{1,0:T(4,128)(2,1)S(1)}, bf16[4,7168]{1,0:T(4,128)(2,1)S(1)}, u32[]{:S(2)}, u32[]{:S(2)}) collective-permute-start(bf16[4,7168]{1,0:T(4,128)(2,1)S(1)} %get-tuple-element.40), channel_id=1, source_target_pairs={{0,2},{1,3},{2,0},{3,1},{4,6},{5,7},{6,4},{7,5},{8,10},{9,11},{10,... | collective-permute-start | bytes 172040 | tf_op jit(solution)/shard_map/ppermute | solution.py:473
  112.5 5.8 %collective-permute-start.32 = (bf16[4,7168]{1,0:T(4,128)(2,1)S(1)}, bf16[4,7168]{1,0:T(4,128)(2,1)S(1)}, u32[]{:S(2)}, u32[]{:S(2)}) collective-permute-start(bf16[4,7168]{1,0:T(4,128)(2,1)S(1)} %get-tuple-element.42), channel_id=1, source_target_pairs={{0,4},{1,5},{2,6},{3,7},{4,0},{5,1},{6,2},{7,3},{8,12},{9,13},{10,... | collective-permute-start | bytes 172040 | tf_op jit(solution)/shard_map/ppermute | solution.py:473
  115.1 6.0 %collective-permute-start.33 = (bf16[4,7168]{1,0:T(4,128)(2,1)S(1)}, bf16[4,7168]{1,0:T(4,128)(2,1)S(1)}, u32[]{:S(2)}, u32[]{:S(2)}) collective-permute-start(bf16[4,7168]{1,0:T(4,128)(2,1)S(1)} %get-tuple-element.41), channel_id=1, source_target_pairs={{0,6},{1,7},{2,4},{3,5},{4,2},{5,3},{6,0},{7,1},{8,14},{9,15},{10,... | collective-permute-start | bytes 172040 | tf_op jit(solution)/shard_map/ppermute | solution.py:473
  (13 other events, 195.8 us)
